TPU v7x, 512 devices: a whole 4x4x16 slice. The times are simulated.
512 devices in a mesh: seq: 32 (over x_hi, z), head: 16 (over x_lo, y, core).
Axes of the slice: x: 4 (x_hi: 2, x_lo: 2; x = x_hi * 2 + x_lo), y: 4, z: 16, core: 2. Of those that a mesh axis runs over, the one named last changes fastest.
Arguments:
- tokens: bfloat16 [8192, 4608], P('seq', 'head'), may hold values from -32 to 32
- segments: int32 [8192], P('seq'), may hold values from 0 to 7, never falling along the last dimension, each value on 1 to 4096 neighbouring positions
- pre_gain: float32 [4608], replicated, may hold values from 0.1 to 1.9
- post_gain: float32 [4608], replicated, may hold values from 0.1 to 1.9
- w_query: bfloat16 [4608, 4096], P('seq', 'head'), may hold values from -0.375 to 0.375
- w_key: bfloat16 [4608, 2048], P('seq', 'head'), may hold values from -0.1875 to 0.1875
- w_value: bfloat16 [4608, 2048], P('seq', 'head'), may hold values from -0.09375 to 0.09375
- w_out: bfloat16 [4096, 4608], P('head', 'seq'), may hold values from -0.09375 to 0.09375
Outputs:
- mixed: bfloat16 [8192, 4608], P('seq')
Inputs may be any that keep to these rules, and one draw needn't show every extreme that they name: `segments`: segment ids never fall; each of the 8 documents holds at least one token and at most 4096, one exactly 4096.
All inputs are finite; a program needn't handle non-finite values.
Results may differ from a plain program's by a relative error of at most 0.01.
Values may be sent and summed in bfloat16 or wider, within the bound.
No kernel may reach another device: no remote copies, remote signals or barrier semaphores. Data moves between devices by JAX's collectives and lax.ppermute only.
A program may use at most 64 MiB of HBM per device.

v0:
```python
import jax
import jax.numpy as jnp
from jax import lax
from jax.experimental import pallas as pl
from jax.experimental.pallas import tpu as pltpu
from jax.sharding import Mesh
from jax.sharding import PartitionSpec as P

D = 4608
HD = 128
GROUP = 2
SCALAR = 144
DOCS = 8
SEQ = ("xh", "z")
HEAD = ("xl", "y", "c")
PLANE = ("xl", "y")

EPS = 1e-06
CAP = 50.0


def from_everyone(shard, axis):
    copies = jnp.broadcast_to(shard, (lax.axis_size(axis), *shard.shape))
    return lax.all_to_all(copies, axis, split_axis=0, concat_axis=0, tiled=True)


def rotate(values, cosine, sine):
    half = values.shape[1] // 2
    first = values[:, :half]
    second = values[:, half:]
    return jnp.concatenate(
        [first * cosine - second * sine, second * cosine + first * sine], axis=1
    )


def attend_kernel(
    where_ref, query_ref, start_ref, kv_hbm, near_ref, away_ref, held, sums, total, sem
):
    rows = query_ref.shape[0] // GROUP
    low = where_ref[0]
    own = where_ref[1]
    halves = where_ref[2]

    def fetch(j):
        place = (lax.rem(j, halves) * 2 + lax.div(j, halves)) * rows
        return pltpu.make_async_copy(
            kv_hbm.at[pl.ds(pl.multiple_of(place, rows), rows), :], held.at[j], sem.at[j]
        )

    @pl.loop(low, own + 1)
    def _(j):
        fetch(j).start()

    sums[...] = jnp.zeros_like(sums)
    total[...] = jnp.zeros_like(total)

    def gather(j, count, masked):
        for k in range(count):
            fetch(j + k).wait()
        keys = held[pl.ds(j, count), :, :HD].reshape(count * rows, HD)
        values = held[pl.ds(j, count), :, HD:].reshape(count * rows, HD)
        scores = lax.dot_general(
            query_ref[...], keys, (((1,), (1,)), ((), ())), preferred_element_type=jnp.float32
        )
        weights = jnp.exp(CAP * jnp.tanh(scores * (1.0 / CAP)))
        if masked:
            shape = (GROUP * rows, rows)
            row = lax.broadcasted_iota(jnp.int32, shape, 0)
            index = own * rows + jnp.where(row >= rows, row - rows, row)
            key_index = j * rows + lax.broadcasted_iota(jnp.int32, shape, 1)
            allowed = (key_index >= start_ref[...]) & (key_index <= index)
            weights = jnp.where(allowed, weights, 0.0)
        part = weights[:, :HD]
        for k in range(1, count * rows // HD):
            part = part + weights[:, k * HD : (k + 1) * HD]
        sums[...] += part
        total[...] += jnp.dot(
            weights.astype(jnp.bfloat16), values, preferred_element_type=jnp.float32
        )

    done = low + 1
    for count in (4, 2, 1):
        steps = lax.div(jnp.maximum(own - done, 0), count)

        @pl.loop(0, steps)
        def _(i, done=done, count=count):
            gather(done + i * count, count, False)

        done = done + steps * count

    seen = start_ref[...] < own * rows
    sums[...] = jnp.where(seen, sums[...], 0.0)
    total[...] = jnp.where(seen, total[...], 0.0)

    @pl.when(low < own)
    def _():
        gather(low, 1, True)

    gather(own, 1, True)

    result = total[...] / jnp.sum(sums[...], axis=1, keepdims=True)
    south = where_ref[3] == 0
    for k in range(GROUP):
        upper = result[k * rows : k * rows + rows // 2]
        lower = result[k * rows + rows // 2 : (k + 1) * rows]
        columns = slice(k * HD, (k + 1) * HD)
        near_ref[:, columns] = jnp.where(south, upper, lower).astype(jnp.bfloat16)
        away_ref[:, columns] = jnp.where(south, lower, upper).astype(jnp.bfloat16)


def attend(where, stacked, starts, kv):
    rows = stacked.shape[0] // GROUP
    blocks = kv.shape[0] // rows
    vmem = pl.BlockSpec(memory_space=pltpu.VMEM)
    return pl.pallas_call(
        attend_kernel,
        out_shape=[jax.ShapeDtypeStruct((rows // 2, GROUP * HD), jnp.bfloat16)] * 2,
        in_specs=[
            pl.BlockSpec(memory_space=pltpu.SMEM),
            vmem,
            vmem,
            pl.BlockSpec(memory_space=pltpu.HBM),
        ],
        out_specs=[vmem, vmem],
        scratch_shapes=[
            pltpu.VMEM((blocks, rows, 2 * HD), jnp.bfloat16),
            pltpu.VMEM((GROUP * rows, HD), jnp.float32),
            pltpu.VMEM((GROUP * rows, HD), jnp.float32),
            pltpu.SemaphoreType.DMA((blocks,)),
        ],
        compiler_params=pltpu.CompilerParams(vmem_limit_bytes=54 * 1024 * 1024),
        cost_estimate=pl.CostEstimate(
            flops=4 * GROUP * rows * HD * kv.shape[0] // 2,
            bytes_accessed=kv.size,
            transcendentals=GROUP * rows * kv.shape[0],
        ),
    )(where, stacked, starts, kv)


def finish_kernel(side_ref, part_ref, both_ref, cos_ref, sin_ref, out_ref):
    other = jnp.where(side_ref[0] == 0, both_ref[1], both_ref[0])
    keys = part_ref[:, :HD] + other[:, :HD].astype(jnp.float32)
    turned = keys * cos_ref[...] + pltpu.roll(keys, HD // 2, 1) * sin_ref[...]
    out_ref[:, :HD] = turned.astype(jnp.bfloat16)
    values = part_ref[:, HD:] + other[:, HD:].astype(jnp.float32)
    out_ref[:, HD:] = values.astype(jnp.bfloat16)


def finish(side, part, both, cosine, sine):
    vmem = pl.BlockSpec(memory_space=pltpu.VMEM)
    return pl.pallas_call(
        finish_kernel,
        out_shape=jax.ShapeDtypeStruct(part.shape, jnp.bfloat16),
        in_specs=[pl.BlockSpec(memory_space=pltpu.SMEM), vmem, vmem, vmem, vmem],
        out_specs=vmem,
        compiler_params=pltpu.CompilerParams(vmem_limit_bytes=16 * 1024 * 1024),
    )(side, part, both, cosine, sine)


def local(tokens, segments, pre_gain, post_gain, w_query, w_key, w_value, w_out):
    rows, width = tokens.shape
    deep = lax.axis_size("z")
    mine = jnp.concatenate([w_key, w_value, w_query, w_out.T], axis=1)
    weights = lax.all_gather(mine, "z", axis=0, tiled=True)
    deep_half = weights.shape[0]

    ids = jnp.broadcast_to(segments.astype(jnp.bfloat16)[None, :], (16, rows))
    slices = jnp.concatenate([tokens.T, ids], axis=0)
    slices = lax.ppermute(slices, ("xh", "xl"), [(0, 0), (1, 2), (2, 1), (3, 3)])
    slices = from_everyone(slices[None], PLANE).reshape(-1, *slices.shape)
    slices = from_everyone(slices[None], "c").reshape(2, 2, -1, *slices.shape[1:])
    seg = slices[0, :, 0, width].astype(jnp.float32)
    levels = jnp.arange(DOCS, dtype=jnp.float32)
    counts = jnp.sum((levels[:, None, None] > seg[None]).astype(jnp.float32), axis=(1, 2))
    starts = jnp.sum(from_everyone(counts[None], "z").reshape(-1, DOCS), axis=0)
    onehot = (seg[:, :, None] == levels).astype(jnp.float32)
    tok_start = jnp.sum(onehot * starts, axis=2)
    side = lax.axis_index("xh")
    place = lax.axis_index("z")
    blocks = (jnp.arange(2, dtype=jnp.int32) * deep + place)[:, None] * rows
    index_f = (blocks + jnp.arange(rows, dtype=jnp.int32)).astype(jnp.float32)
    position = (index_f - tok_start).reshape(2 * rows)
    half = HD // 2
    freq = 10000.0 ** (-(jnp.arange(half, dtype=jnp.float32) / half))
    angle = position[:, None] * freq[None, :]
    cosine, sine = jnp.cos(angle), jnp.sin(angle)
    start_i = lax.dynamic_index_in_dim(tok_start, side, 0, keepdims=False).astype(jnp.int32)
    where = jnp.stack(
        [
            start_i[0] // rows,
            (side * deep + place).astype(jnp.int32),
            jnp.int32(deep),
            lax.axis_index("c").astype(jnp.int32),
        ]
    )
    starts_col = jnp.tile(start_i, GROUP)[:, None]

    wide = slices[:, :, :, :width].transpose(1, 2, 0, 3, 4).reshape(2, deep_half, rows)
    wide = wide.astype(jnp.float32)
    squares = jnp.sum(lax.all_gather(jnp.sum(wide * wide, axis=1), "xh", axis=0), axis=0)
    scale = lax.rsqrt(squares / D + EPS)
    gain = lax.dynamic_slice_in_dim(pre_gain, side * deep_half, deep_half, 0)
    normed = (wide * scale[:, None, :] * gain[None, :, None]).astype(jnp.bfloat16)
    normed = normed.transpose(0, 2, 1).reshape(2 * rows, deep_half)
    near = lax.axis_size(PLANE)
    few = rows // (near * 2)
    pieces = tokens.reshape(2, near, few, width).transpose(1, 0, 2, 3).reshape(-1, few, width)
    own = lax.all_to_all(pieces, HEAD, 0, 0, tiled=True).transpose(1, 0, 2).reshape(few, D)
    cos_wide = jnp.concatenate([cosine, cosine], axis=1)
    sin_wide = jnp.concatenate([-sine, sine], axis=1)
    normed, cosine, sine, cos_wide, sin_wide, weights, own = lax.optimization_barrier(
        (normed, cosine, sine, cos_wide, sin_wide, weights, own)
    )

    def project(columns):
        return jnp.dot(normed, columns, preferred_element_type=jnp.float32)

    part = project(weights[:, : 2 * HD])
    both = lax.all_gather(part.astype(jnp.bfloat16), "xh", axis=0)
    kv_pair = finish(side.astype(jnp.int32)[None], part, both, cos_wide, sin_wide)
    kv_pair, weights = lax.optimization_barrier((kv_pair, weights))
    kv_all = lax.all_gather(kv_pair, "z", axis=0, tiled=True)

    query = project(weights[:, 2 * HD : 4 * HD]).reshape(2, rows, 2 * HD)
    query = jnp.sum(lax.all_to_all(query, "xh", 0, 0, tiled=True), axis=0)
    own_cos = lax.dynamic_slice_in_dim(cosine, side * rows, rows, 0)
    own_sin = lax.dynamic_slice_in_dim(sine, side * rows, rows, 0)
    stacked = jnp.concatenate(
        [
            (rotate(query[:, k * HD : (k + 1) * HD], own_cos, own_sin) * SCALAR ** (-0.5)).astype(
                jnp.bfloat16
            )
            for k in range(GROUP)
        ],
        axis=0,
    )
    out_t = from_everyone(weights[None, :, 4 * HD :], "xh").reshape(D, GROUP * HD)
    swap = [(0, 1), (1, 0)]
    out_far = lax.ppermute(out_t, "c", swap)
    kv_all, stacked, out_t, out_far = lax.optimization_barrier((kv_all, stacked, out_t, out_far))

    kept, away = attend(where, stacked, starts_col, kv_all)
    far = lax.ppermute(away, "c", swap)

    def through(part, rows_of):
        return lax.dot_general(
            part, rows_of, (((1,), (1,)), ((), ())), preferred_element_type=jnp.float32
        )

    near_part = through(kept, out_t)
    near_part, far = lax.optimization_barrier((near_part, far))
    halves = (near_part + through(far, out_far)).astype(jnp.bfloat16)
    pieces = lax.all_to_all(halves.reshape(near, few, D), PLANE, 0, 0, tiled=True)
    proj = jnp.sum(pieces.astype(jnp.float32), axis=0)
    post = lax.rsqrt(jnp.mean(proj * proj, axis=1, keepdims=True) + EPS)
    result = (own.astype(jnp.float32) + proj * post * post_gain[None, :]).astype(jnp.bfloat16)
    result = from_everyone(result, PLANE).reshape(rows // 2, D)
    other = lax.ppermute(result, "c", swap)
    mine_first = (jnp.arange(2) == lax.axis_index("c"))[:, None, None]
    return jnp.where(mine_first, result[None], other[None]).reshape(rows, D)


def solution(mesh):
    finer = Mesh(mesh.devices.reshape(2, 16, 2, 4, 2), ("xh", "z", "xl", "y", "c"))
    in_specs = (
        P(SEQ, HEAD),
        P(SEQ),
        P(),
        P(),
        P(SEQ, HEAD),
        P(SEQ, HEAD),
        P(SEQ, HEAD),
        P(HEAD, SEQ),
    )
    return jax.shard_map(
        local, mesh=finer, in_specs=in_specs, out_specs=P(SEQ, None), check_vma=False
    )
```

profile of v0, /device:TPU:1, one launch (start us, length us, event | category | flops | bytes accessed | tf_op | source)
XLA Modules:
  0.0 247.4 jit_solution(3272712311873392273)
XLA Ops:
  6.5 1.6 pad_maximum_fusion.2
  8.2 0.7 convert_element_type.71
  8.9 0.9 pad_maximum_fusion.3
  9.8 0.7 collective-permute-start
  10.5 1.1 copy.33
  11.6 16.1 %all_to_all.40 = bf16[16,16,288]{2,1,0:T(8,128)(2,1)S(1)} all-to-all(bf16[16,16,288]{2,1,0:T(8,128)(2,1)S(1)} %bitcast.68), channel_id=1, replica_groups=mesh['xh'=2,'z'=16,'xl'=2,'y'=4,'c'=2] {'xl','y','c'}, dimensions={0} | all-to-all | bytes 294912 | tf_op jit(solution)/shard_map/all_to_all | solution.py:208
  27.7 1.1 broadcast_in_dim.79
  28.8 3.6 %all-to-all-start = ((bf16[8,1,304,256]{3,2,1,0:T(8,128)(2,1)}), bf16[8,1,304,256]{3,2,1,0:T(8,128)(2,1)S(1)}, u32[]{:S(2)}, u32[]{:S(2)}) async-start(bf16[8,1,304,256]{3,2,1,0:T(8,128)(2,1)} %broadcast_in_dim.79), calls=%async_computation | async-start | bytes 2490368 | tf_op jit(solution)/shard_map/all_to_all | solution.py:24
  32.4 0.1 dynamic_slice.13
  32.6 0.9 reshape.112
  33.4 16.1 %all-to-all-done = bf16[8,1,304,256]{3,2,1,0:T(8,128)(2,1)S(1)} async-done(((bf16[8,1,304,256]{3,2,1,0:T(8,128)(2,1)}), bf16[8,1,304,256]{3,2,1,0:T(8,128)(2,1)S(1)}, u32[]{:S(2)}, u32[]{:S(2)}) %all-to-all-start) | async-done | bytes 1245216 | tf_op jit(solution)/shard_map/all_to_all | solution.py:24
  49.5 0.2 broadcast_in_dim.80
  49.7 6.0 %all_to_all.41 = bf16[2,1,8,304,256]{4,3,2,1,0:T(8,128)(2,1)S(1)} all-to-all(bf16[2,1,8,304,256]{4,3,2,1,0:T(8,128)(2,1)S(1)} %broadcast_in_dim.80), channel_id=1, replica_groups=mesh['xh'=2,'z'=16,'xl'=2,'y'=4,'c'=2] {'c'}, dimensions={0} | all-to-all | bytes 4980736 | tf_op jit(solution)/shard_map/all_to_all | solution.py:24
  55.7 0.2 copy.30
  55.9 0.1 convert_reduce_fusion.1
  56.0 0.6 broadcast_in_dim.81
  56.6 14.9 %all-to-all-start.2 = ((f32[16,1,8]{2,1,0:T(1,128)}), f32[16,1,8]{2,1,0:T(1,128)S(1)}, u32[]{:S(2)}, u32[]{:S(2)}) async-start(f32[16,1,8]{2,1,0:T(1,128)} %broadcast_in_dim.81), calls=%async_computation.2 | async-start | bytes 16384 | tf_op jit(solution)/shard_map/all_to_all | solution.py:24
  71.5 0.0 all-gather.8.cloned.1.call-start
  71.6 0.5 multiply_reduce_fusion
  72.1 4.7 %all-gather.2 = f32[2,2,256]{2,1,0:T(2,128)S(1)} all-gather(f32[1,2,256]{2,1,0:T(2,128)S(1)} %bitcast.78), channel_id=2, replica_groups=mesh['xh'=2,'z'=16,'xl'=2,'y'=4,'c'=2] {'xh'}, dimensions={0}, use_global_device_ids=true | all-gather | bytes 6144 | tf_op jit(solution)/shard_map/all_gather | solution.py:200
  76.8 0.5 slice_convert_fusion
  77.3 0.8 fusion.1
  78.1 2.4 copy.31
  80.6 2.2 all-to-all-done.2
  82.8 0.1 select_reduce_fusion
  82.9 0.1 subtract_bitcast_fusion
  83.0 1.0 fusion.8
  84.0 0.7 copy-done
  84.7 0.1 copy-done.2
  84.8 0.2 pad_maximum_fusion
  85.0 0.0 all-gather.6.cloned.1.call-done
  85.0 2.8 %fusion.9 = (bf16[512,256]{1,0:T(8,128)(2,1)S(1)}, f32[512,256]{1,0:T(8,128)S(1)}) fusion(bf16[512,2304]{1,0:T(8,128)(2,1)} %bitcast.65, bf16[2304,768]{1,0:T(8,128)(2,1)} %all-gather.6.cloned.1.call-done), kind=kOutput, calls=%fused_computation.46 | convolution fusion | flops 604110848 | bytes 4325376 | tf_op jit(solution)/shard_map/dot_general | solution.py:216
  87.8 7.4 %all-gather.1 = bf16[1024,256]{1,0:T(8,128)(2,1)S(1)} all-gather(bf16[512,256]{1,0:T(8,128)(2,1)S(1)} %get-tuple-element.46), channel_id=3, replica_groups=mesh['xh'=2,'z'=16,'xl'=2,'y'=4,'c'=2] {'xh'}, dimensions={0}, use_global_device_ids=true | all-gather | bytes 786432 | tf_op jit(solution)/shard_map/all_gather | solution.py:219
  95.2 0.8 shard_map.82
  96.1 0.5 slice-done
  96.5 0.2 broadcast_in_dim.83
  96.7 20.7 %all_to_all.42 = bf16[2,1,2304,256]{3,2,1,0:T(8,128)(2,1)S(1)} all-to-all(bf16[2,1,2304,256]{3,2,1,0:T(8,128)(2,1)S(1)} %broadcast_in_dim.83), channel_id=1, replica_groups=mesh['xh'=2,'z'=16,'xl'=2,'y'=4,'c'=2] {'xh'}, dimensions={0} | all-to-all | bytes 4718592 | tf_op jit(solution)/shard_map/all_to_all | solution.py:24
  117.4 13.8 %collective-permute-start.1 = (bf16[4608,256]{1,0:T(8,128)(2,1)S(1)}, bf16[4608,256]{1,0:T(8,128)(2,1)}, u32[]{:S(2)}, u32[]{:S(2)}) collective-permute-start(bf16[4608,256]{1,0:T(8,128)(2,1)S(1)} %bitcast.58), channel_id=1, source_target_pairs={{0,1},{1,0},{2,3},{3,2},{4,5},{5,4},{6,7},{7,6},{8,9},{9,8},{10,11... | collective-permute-start | bytes 7077896 | tf_op jit(solution)/shard_map/ppermute | solution.py:239
  131.3 0.6 slice.49
  134.4 3.6 %fusion.2 = f32[512,256]{1,0:T(8,128)} fusion(bf16[512,2304]{1,0:T(8,128)(2,1)} %bitcast.66, bf16[2304,768]{1,0:T(8,128)(2,1)} %all-gather.6.cloned.1.call-done), kind=kOutput, calls=%fused_computation.8 | convolution fusion | flops 603979776 | bytes 4063232 | tf_op jit(solution)/shard_map/dot_general | solution.py:216
  138.1 3.5 %all-to-all-start.4 = ((f32[2,256,256]{2,1,0:T(8,128)}), f32[2,256,256]{2,1,0:T(8,128)S(1)}, u32[]{:S(2)}, u32[]{:S(2)}) async-start(f32[2,256,256]{2,1,0:T(8,128)} %bitcast.71), calls=%async_computation.4 | async-start | bytes 1048576 | tf_op jit(solution)/shard_map/all_to_all | solution.py:225
  141.6 0.9 copy.41
  142.5 0.6 pad_add_fusion.where_ref
  143.1 8.0 %all-to-all-done.4 = f32[2,256,256]{2,1,0:T(8,128)S(1)} async-done(((f32[2,256,256]{2,1,0:T(8,128)}), f32[2,256,256]{2,1,0:T(8,128)S(1)}, u32[]{:S(2)}, u32[]{:S(2)}) %all-to-all-start.4) | async-done | bytes 524320 | tf_op jit(solution)/shard_map/all_to_all | solution.py:225
  151.1 1.0 multiply_subtract_fusion.1
  152.2 0.1 fusion.7
  152.3 0.1 fusion.6
  152.4 0.7 pad_maximum_fusion.4.query_ref
  153.1 19.0 %all-gather.8.cloned.1.call-done.kv_hbm = bf16[8192,256]{1,0:T(8,128)(2,1)} async-done(((bf16[512,256]{1,0:T(8,128)(2,1)}), bf16[8192,256]{1,0:T(8,128)(2,1)}) %all-gather.8.cloned.1.call-update) | async-done | bytes 4194320 | tf_op jit(solution)/shard_map/all_gather | solution.py:222
  172.0 3.4 %shard_map.83 = (bf16[128,256]{1,0:T(8,128)(2,1)}, bf16[128,256]{1,0:T(8,128)(2,1)}) custom-call(s32[4]{0:T(128)} %pad_add_fusion.where_ref, bf16[512,128]{1,0:T(8,128)(2,1)} %pad_maximum_fusion.4.query_ref, s32[512,1]{1,0:T(8,128)} %bitcast.72, bf16[8192,256]{1,0:T(8,128)(2,1)} %all-gather.8.cloned.1.call-done.kv_hbm), custom_call_target="tpu_custom_call" | custom-call | flops 1073741824 | bytes 2097152 | tf_op jit(solution)/shard_map/pallas_call | solution.py:115
  175.4 11.0 %collective-permute-start.2 = (bf16[128,256]{1,0:T(8,128)(2,1)}, bf16[128,256]{1,0:T(8,128)(2,1)S(1)}, u32[]{:S(2)}, u32[]{:S(2)}) collective-permute-start(bf16[128,256]{1,0:T(8,128)(2,1)} %get-tuple-element.35), channel_id=1, source_target_pairs={{0,1},{1,0},{2,3},{3,2},{4,5},{5,4},{6,7},{7,6},{8,9},{9,8},{10,11... | collective-permute-start | bytes 196616 | tf_op jit(solution)/shard_map/ppermute | solution.py:243
  186.4 1.7 fusion.10
  188.1 2.6 %fusion.11 = f32[128,4608]{1,0:T(8,128)S(1)} fusion(bf16[128,256]{1,0:T(8,128)(2,1)S(1)} %collective-permute-done.2, bf16[4608,256]{1,0:T(8,128)(2,1)} %collective-permute-done.1), kind=kOutput, calls=%fused_computation.48 | convolution fusion | flops 301989888 | bytes 4784128 | tf_op jit(solution)/shard_map/dot_general | solution.py:246
  190.7 0.2 add_convert_fusion
  190.9 21.4 %all_to_all.43 = bf16[8,16,4608]{2,1,0:T(8,128)(2,1)S(1)} all-to-all(bf16[8,16,4608]{2,1,0:T(8,128)(2,1)S(1)} %bitcast.64), channel_id=1, replica_groups=mesh['xh'=2,'z'=16,'xl'=2,'y'=4,'c'=2] {'xl','y'}, dimensions={0} | all-to-all | bytes 2359296 | tf_op jit(solution)/shard_map/all_to_all | solution.py:253
  212.3 0.2 convert_reduce_fusion
  212.5 0.2 multiply_reduce_fusion.1
  212.6 0.1 add_convert_fusion.1
  212.8 0.1 broadcast_in_dim.84
  212.8 19.7 %all_to_all.44 = bf16[8,16,4608]{2,1,0:T(8,128)(2,1)S(1)} all-to-all(bf16[8,16,4608]{2,1,0:T(8,128)(2,1)S(1)} %broadcast_in_dim.84), channel_id=1, replica_groups=mesh['xh'=2,'z'=16,'xl'=2,'y'=4,'c'=2] {'xl','y'}, dimensions={0} | all-to-all | bytes 2359296 | tf_op jit(solution)/shard_map/all_to_all | solution.py:24
  232.6 3.8 %collective-permute-start.3 = (bf16[128,4608]{1,0:T(8,128)(2,1)S(1)}, bf16[128,4608]{1,0:T(8,128)(2,1)S(1)}, u32[]{:S(2)}, u32[]{:S(2)}) collective-permute-start(bf16[128,4608]{1,0:T(8,128)(2,1)S(1)} %bitcast.62), channel_id=1, source_target_pairs={{0,1},{1,0},{2,3},{3,2},{4,5},{5,4},{6,7},{7,6},{8,9},{9,8},{10,11... | collective-permute-start | bytes 3538952 | tf_op jit(solution)/shard_map/ppermute | solution.py:258
  236.5 0.1 broadcast_bitcast_fusion.1
  236.5 2.4 collective-permute-done.3
  238.9 1.7 bitcast_select_fusion
  (34 shorter events, 0.3 us)
Async XLA Ops:
  6.5 78.5 %all-gather.6.cloned.1.call-start = ((), (), s32[]{:S(2)}) async-start(), calls=%async_computation.8 | async-start | bytes 3760128 | tf_op jit(solution)/shard_map/all_gather | solution.py:164
  9.8 17.9 %collective-permute-start = (bf16[304,256]{1,0:T(8,128)(2,1)S(1)}, bf16[304,256]{1,0:T(8,128)(2,1)S(1)}, u32[]{:S(2)}, u32[]{:S(2)}) collective-permute-start(bf16[304,256]{1,0:T(8,128)(2,1)S(1)} %pad_maximum_fusion.3), channel_id=1, source_target_pairs={{0,0},{8,256},{256,8},{264,264},{1,1},{9,257},{257,9},{265,265},{2... | collective-permute-start | bytes 466952 | tf_op jit(solution)/shard_map/ppermute | solution.py:169
  11.6 20.8 %copy-start.5 = (f32[4608]{0:T(1024)S(1)}, f32[4608]{0:T(1024)}, u32[]{:S(2)}) copy-start(f32[4608]{0:T(1024)} %param.10) | copy-start | bytes 55300
  28.8 20.7 %all-to-all-start = ((bf16[8,1,304,256]{3,2,1,0:T(8,128)(2,1)}), bf16[8,1,304,256]{3,2,1,0:T(8,128)(2,1)S(1)}, u32[]{:S(2)}, u32[]{:S(2)}) async-start(bf16[8,1,304,256]{3,2,1,0:T(8,128)(2,1)} %broadcast_in_dim.79), calls=%async_computation | async-start | bytes 2490368 | tf_op jit(solution)/shard_map/all_to_all | solution.py:24
  56.6 26.2 %all-to-all-start.2 = ((f32[16,1,8]{2,1,0:T(1,128)}), f32[16,1,8]{2,1,0:T(1,128)S(1)}, u32[]{:S(2)}, u32[]{:S(2)}) async-start(f32[16,1,8]{2,1,0:T(1,128)} %broadcast_in_dim.81), calls=%async_computation.2 | async-start | bytes 16384 | tf_op jit(solution)/shard_map/all_to_all | solution.py:24
  71.5 100.5 %all-gather.8.cloned.1.call-start = ((), (), s32[]{:S(2)}) async-start(), calls=%async_computation.9 | async-start | bytes 4456448 | tf_op jit(solution)/shard_map/all_gather | solution.py:222
  84.0 0.7 copy-start
  84.0 0.8 copy-start.2
  95.2 1.4 slice-start
  117.4 35.6 %collective-permute-start.1 = (bf16[4608,256]{1,0:T(8,128)(2,1)S(1)}, bf16[4608,256]{1,0:T(8,128)(2,1)}, u32[]{:S(2)}, u32[]{:S(2)}) collective-permute-start(bf16[4608,256]{1,0:T(8,128)(2,1)S(1)} %bitcast.58), channel_id=1, source_target_pairs={{0,1},{1,0},{2,3},{3,2},{4,5},{5,4},{6,7},{7,6},{8,9},{9,8},{10,11... | collective-permute-start | bytes 7077896 | tf_op jit(solution)/shard_map/ppermute | solution.py:239
  134.4 16.7 %copy-start.1 = (f32[512,64]{1,0:T(8,128)S(1)}, f32[512,64]{1,0:T(8,128)}, u32[]{:S(2)}) copy-start(f32[512,64]{1,0:T(8,128)} %copy-done) | copy-start | bytes 393220
  138.1 13.0 %all-to-all-start.4 = ((f32[2,256,256]{2,1,0:T(8,128)}), f32[2,256,256]{2,1,0:T(8,128)S(1)}, u32[]{:S(2)}, u32[]{:S(2)}) async-start(f32[2,256,256]{2,1,0:T(8,128)} %bitcast.71), calls=%async_computation.4 | async-start | bytes 1048576 | tf_op jit(solution)/shard_map/all_to_all | solution.py:225
  175.4 12.7 %collective-permute-start.2 = (bf16[128,256]{1,0:T(8,128)(2,1)}, bf16[128,256]{1,0:T(8,128)(2,1)S(1)}, u32[]{:S(2)}, u32[]{:S(2)}) collective-permute-start(bf16[128,256]{1,0:T(8,128)(2,1)} %get-tuple-element.35), channel_id=1, source_target_pairs={{0,1},{1,0},{2,3},{3,2},{4,5},{5,4},{6,7},{7,6},{8,9},{9,8},{10,11... | collective-permute-start | bytes 196616 | tf_op jit(solution)/shard_map/ppermute | solution.py:243
  190.9 21.7 %copy-start.3 = (bf16[16,4608]{1,0:T(8,128)(2,1)S(1)}, bf16[16,4608]{1,0:T(8,128)(2,1)}, u32[]{:S(2)}) copy-start(bf16[16,4608]{1,0:T(8,128)(2,1)} %reshape.112) | copy-start | bytes 442372
  190.9 21.7 %copy-start.4 = (f32[4608]{0:T(1024)S(1)}, f32[4608]{0:T(1024)}, u32[]{:S(2)}) copy-start(f32[4608]{0:T(1024)} %param.11) | copy-start | bytes 55300
  232.6 6.3 %collective-permute-start.3 = (bf16[128,4608]{1,0:T(8,128)(2,1)S(1)}, bf16[128,4608]{1,0:T(8,128)(2,1)S(1)}, u32[]{:S(2)}, u32[]{:S(2)}) collective-permute-start(bf16[128,4608]{1,0:T(8,128)(2,1)S(1)} %bitcast.62), channel_id=1, source_target_pairs={{0,1},{1,0},{2,3},{3,2},{4,5},{5,4},{6,7},{7,6},{8,9},{9,8},{10,11... | collective-permute-start | bytes 3538952 | tf_op jit(solution)/shard_map/ppermute | solution.py:258
Sparse Core Ops, SparseCore 0:
  9.4 73.2 all-gather.5
  96.2 75.8 all-gather.7
where the time goes:
time: 250 us; the launch traced here: 247 us
  blocking collectives  96 us (38%)
  starting transfers between devices  51.3 us (21%)
  waiting for transfers between devices  47.7 us (19%)
  between operations  16.3 us (7%)
  other arithmetic  11.5 us (5%)
  matrix products  10.7 us (4%)
  local copies, waits for them, and re-layouts  9.62 us (4%)
  Pallas kernels  4.21 us (2%)
    all_to_all x3, blocking collectives, from_everyone(): return lax.all_to_all(copies, axis, split_axis=0, concat_axis=0, tiled=True)  46.5 us
    all_to_all x1, blocking collectives, local(): lax.all_to_all(halves.reshape(near, few, D), PLANE, 0, 0, tiled=True)  21.4 us
    all_gather x1, waiting for transfers between devices, local(): kv_all = lax.all_gather(kv_pair, 'z', axis=0, tiled=True)  19 us
    all_to_all x2, starting transfers between devices, from_everyone(): return lax.all_to_all(copies, axis, split_axis=0, concat_axis=0, tiled=True)  18.5 us
    all_to_all x2, waiting for transfers between devices, from_everyone(): return lax.all_to_all(copies, axis, split_axis=0, concat_axis=0, tiled=True)  18.3 us
    all_to_all x1, blocking collectives, local(): lax.all_to_all(pieces, HEAD, 0, 0, tiled=True).transpose(1, 0, 2)  16.1 us
    ppermute x1, starting transfers between devices, local(): out_far = lax.ppermute(out_t, 'c', swap)  13.8 us
    ppermute x1, starting transfers between devices, local(): far = lax.ppermute(away, 'c', swap)  11 us
  transfers between devices with their start and end apart: 9, of which 5 were waited for; matrix products, arithmetic and copies ran while one was open for 9% of the time, Pallas kernels for 0%

commit v1 on v0

--- a/solution.py
+++ b/solution.py
@@ -202,14 +202,10 @@
     gain = lax.dynamic_slice_in_dim(pre_gain, side * deep_half, deep_half, 0)
     normed = (wide * scale[:, None, :] * gain[None, :, None]).astype(jnp.bfloat16)
     normed = normed.transpose(0, 2, 1).reshape(2 * rows, deep_half)
-    near = lax.axis_size(PLANE)
-    few = rows // (near * 2)
-    pieces = tokens.reshape(2, near, few, width).transpose(1, 0, 2, 3).reshape(-1, few, width)
-    own = lax.all_to_all(pieces, HEAD, 0, 0, tiled=True).transpose(1, 0, 2).reshape(few, D)
     cos_wide = jnp.concatenate([cosine, cosine], axis=1)
     sin_wide = jnp.concatenate([-sine, sine], axis=1)
-    normed, cosine, sine, cos_wide, sin_wide, weights, own = lax.optimization_barrier(
-        (normed, cosine, sine, cos_wide, sin_wide, weights, own)
+    normed, cosine, sine, cos_wide, sin_wide, weights = lax.optimization_barrier(
+        (normed, cosine, sine, cos_wide, sin_wide, weights)
     )
 
     def project(columns):
@@ -218,7 +214,7 @@
     part = project(weights[:, : 2 * HD])
     both = lax.all_gather(part.astype(jnp.bfloat16), "xh", axis=0)
     kv_pair = finish(side.astype(jnp.int32)[None], part, both, cos_wide, sin_wide)
-    kv_pair, weights = lax.optimization_barrier((kv_pair, weights))
+    kv_pair, weights, tokens = lax.optimization_barrier((kv_pair, weights, tokens))
     kv_all = lax.all_gather(kv_pair, "z", axis=0, tiled=True)
 
     query = project(weights[:, 2 * HD : 4 * HD]).reshape(2, rows, 2 * HD)
@@ -235,9 +231,15 @@
         axis=0,
     )
     out_t = from_everyone(weights[None, :, 4 * HD :], "xh").reshape(D, GROUP * HD)
+    near = lax.axis_size(PLANE)
+    few = rows // (near * 2)
+    pieces = tokens.reshape(2, near, few, width).transpose(1, 0, 2, 3).reshape(-1, few, width)
+    own = lax.all_to_all(pieces, HEAD, 0, 0, tiled=True).transpose(1, 0, 2).reshape(few, D)
     swap = [(0, 1), (1, 0)]
     out_far = lax.ppermute(out_t, "c", swap)
-    kv_all, stacked, out_t, out_far = lax.optimization_barrier((kv_all, stacked, out_t, out_far))
+    kv_all, stacked, out_t, out_far, own = lax.optimization_barrier(
+        (kv_all, stacked, out_t, out_far, own)
+    )
 
     kept, away = attend(where, stacked, starts_col, kv_all)
     far = lax.ppermute(away, "c", swap)

time: 250 us -> 250 us (level)
  starting transfers between devices: 51.3 us -> 67.2 us
  blocking collectives: 96 us -> 80.5 us
    all_to_all x1 -> x0, blocking collectives: 16.1 us -> none  [local(): lax.all_to_all(pieces, HEAD, 0, 0, tiled=True).transpose(1, 0, 2)]
    all_to_all x2, starting transfers between devices: 18.5 us -> 27 us  [from_everyone(): return lax.all_to_all(copies, axis, split_axis=0, concat_axis=0, tiled=True)]
    all_gather x1, waiting for transfers between devices: 19 us -> 11.5 us  [local(): kv_all = lax.all_gather(kv_pair, 'z', axis=0, tiled=True)]
    all_gather x1, waiting for transfers between devices: 0.02 us -> 6.02 us  [local(): weights = lax.all_gather(mine, 'z', axis=0, tiled=True)]
    all_to_all x0 -> x1, starting transfers between devices: none -> 4.49 us  [local(): lax.all_to_all(pieces, HEAD, 0, 0, tiled=True).transpose(1, 0, 2)]
    all_to_all x0 -> x1, waiting for transfers between devices: none -> 3.06 us  [local(): lax.all_to_all(pieces, HEAD, 0, 0, tiled=True).transpose(1, 0, 2)]
    all_to_all x1, waiting for transfers between devices: 7.98 us -> 5.41 us  [local(): query = jnp.sum(lax.all_to_all(query, 'xh', 0, 0, tiled=True), axis=0)]
    ppermute x1, starting transfers between devices: 13.8 us -> 16.4 us  [local(): out_far = lax.ppermute(out_t, 'c', swap)]
  transfers between devices with their start and end apart: 9 -> 10, of which waited for: 5 -> 7; matrix products, arithmetic and copies ran while one was open for 9% -> 9% of each run, Pallas kernels for 0% -> 0%
where the time goes in v1:
time: 250 us; the launch traced here: 248 us
  blocking collectives  80.5 us (32%)
  starting transfers between devices  67.2 us (27%)
  waiting for transfers between devices  47.6 us (19%)
  between operations  16.2 us (6%)
  other arithmetic  11.5 us (5%)
  matrix products  10.6 us (4%)
  local copies, waits for them, and re-layouts  10.3 us (4%)
  Pallas kernels  4.18 us (2%)
    all_to_all x3, blocking collectives, from_everyone(): return lax.all_to_all(copies, axis, split_axis=0, concat_axis=0, tiled=True)  47.1 us
    all_to_all x2, starting transfers between devices, from_everyone(): return lax.all_to_all(copies, axis, split_axis=0, concat_axis=0, tiled=True)  27 us
    all_to_all x1, blocking collectives, local(): lax.all_to_all(halves.reshape(near, few, D), PLANE, 0, 0, tiled=True)  21.2 us
    all_to_all x2, waiting for transfers between devices, from_everyone(): return lax.all_to_all(copies, axis, split_axis=0, concat_axis=0, tiled=True)  19.2 us
    ppermute x1, starting transfers between devices, local(): out_far = lax.ppermute(out_t, 'c', swap)  16.4 us
    all_gather x1, waiting for transfers between devices, local(): kv_all = lax.all_gather(kv_pair, 'z', axis=0, tiled=True)  11.5 us
    ppermute x1, starting transfers between devices, local(): far = lax.ppermute(away, 'c', swap)  11.3 us
    all_gather x1, blocking collectives, local(): both = lax.all_gather(part.astype(jnp.bfloat16), 'xh', axis=0)  7.39 us
  transfers between devices with their start and end apart: 10, of which 7 were waited for; matrix products, arithmetic and copies ran while one was open for 9% of the time, Pallas kernels for 0%

profile of v1, /device:TPU:1, one launch (start us, length us, event | category | flops | bytes accessed | tf_op | source)
XLA Modules:
  0.0 248.0 jit_solution(15178010770771597652)
XLA Ops:
  6.5 1.6 pad_maximum_fusion.2
  8.2 0.7 convert_element_type.71
  8.9 0.9 pad_maximum_fusion.3
  9.8 0.7 collective-permute-start
  10.5 1.1 broadcast_in_dim.80
  11.6 12.0 %all-to-all-start = ((bf16[8,1,304,256]{3,2,1,0:T(8,128)(2,1)}), bf16[8,1,304,256]{3,2,1,0:T(8,128)(2,1)S(1)}, u32[]{:S(2)}, u32[]{:S(2)}) async-start(bf16[8,1,304,256]{3,2,1,0:T(8,128)(2,1)} %broadcast_in_dim.80), calls=%async_computation | async-start | bytes 2490368 | tf_op jit(solution)/shard_map/all_to_all | solution.py:24
  23.7 0.1 dynamic_slice.13
  23.8 16.9 %all-to-all-done = bf16[8,1,304,256]{3,2,1,0:T(8,128)(2,1)S(1)} async-done(((bf16[8,1,304,256]{3,2,1,0:T(8,128)(2,1)}), bf16[8,1,304,256]{3,2,1,0:T(8,128)(2,1)S(1)}, u32[]{:S(2)}, u32[]{:S(2)}) %all-to-all-start) | async-done | bytes 1245216 | tf_op jit(solution)/shard_map/all_to_all | solution.py:24
  40.6 0.2 broadcast_in_dim.81
  40.8 6.3 %all_to_all.40 = bf16[2,1,8,304,256]{4,3,2,1,0:T(8,128)(2,1)S(1)} all-to-all(bf16[2,1,8,304,256]{4,3,2,1,0:T(8,128)(2,1)S(1)} %broadcast_in_dim.81), channel_id=1, replica_groups=mesh['xh'=2,'z'=16,'xl'=2,'y'=4,'c'=2] {'c'}, dimensions={0} | all-to-all | bytes 4980736 | tf_op jit(solution)/shard_map/all_to_all | solution.py:24
  47.1 0.2 copy.30
  47.2 0.1 convert_reduce_fusion.1
  47.4 0.6 broadcast_in_dim.82
  48.0 14.9 %all-to-all-start.2 = ((f32[16,1,8]{2,1,0:T(1,128)}), f32[16,1,8]{2,1,0:T(1,128)S(1)}, u32[]{:S(2)}, u32[]{:S(2)}) async-start(f32[16,1,8]{2,1,0:T(1,128)} %broadcast_in_dim.82), calls=%async_computation.2 | async-start | bytes 16384 | tf_op jit(solution)/shard_map/all_to_all | solution.py:24
  62.9 0.5 multiply_reduce_fusion
  63.5 4.7 %all-gather.2 = f32[2,2,256]{2,1,0:T(2,128)S(1)} all-gather(f32[1,2,256]{2,1,0:T(2,128)S(1)} %bitcast.77), channel_id=2, replica_groups=mesh['xh'=2,'z'=16,'xl'=2,'y'=4,'c'=2] {'xh'}, dimensions={0}, use_global_device_ids=true | all-gather | bytes 6144 | tf_op jit(solution)/shard_map/all_gather | solution.py:200
  68.2 0.5 slice_convert_fusion
  68.7 0.8 fusion.1
  69.5 2.4 copy.31
  71.9 2.3 all-to-all-done.2
  74.3 0.1 select_reduce_fusion
  74.5 1.0 fusion.8
  75.5 0.7 copy-done
  76.2 0.1 copy-done.2
  76.3 0.2 pad_maximum_fusion
  76.5 6.0 %all-gather.6.cloned.1.call-done = bf16[2304,768]{1,0:T(8,128)(2,1)} async-done(((bf16[144,768]{1,0:T(8,128)(2,1)}), bf16[2304,768]{1,0:T(8,128)(2,1)}) %all-gather.6.cloned.1.call-update) | async-done | bytes 3538960 | tf_op jit(solution)/shard_map/all_gather | solution.py:164
  82.5 2.8 %fusion.9 = (bf16[512,256]{1,0:T(8,128)(2,1)S(1)}, f32[512,256]{1,0:T(8,128)S(1)}) fusion(bf16[512,2304]{1,0:T(8,128)(2,1)} %bitcast.65, bf16[2304,768]{1,0:T(8,128)(2,1)} %all-gather.6.cloned.1.call-done), kind=kOutput, calls=%fused_computation.46 | convolution fusion | flops 604110848 | bytes 4325376 | tf_op jit(solution)/shard_map/dot_general | solution.py:212
  85.2 7.4 %all-gather.1 = bf16[1024,256]{1,0:T(8,128)(2,1)S(1)} all-gather(bf16[512,256]{1,0:T(8,128)(2,1)S(1)} %get-tuple-element.48), channel_id=3, replica_groups=mesh['xh'=2,'z'=16,'xl'=2,'y'=4,'c'=2] {'xh'}, dimensions={0}, use_global_device_ids=true | all-gather | bytes 786432 | tf_op jit(solution)/shard_map/all_gather | solution.py:215
  92.6 0.8 shard_map.82
  93.5 0.5 slice-done
  94.0 0.2 broadcast_in_dim.83
  94.2 21.1 %all_to_all.41 = bf16[2,1,2304,256]{3,2,1,0:T(8,128)(2,1)S(1)} all-to-all(bf16[2,1,2304,256]{3,2,1,0:T(8,128)(2,1)S(1)} %broadcast_in_dim.83), channel_id=1, replica_groups=mesh['xh'=2,'z'=16,'xl'=2,'y'=4,'c'=2] {'xh'}, dimensions={0} | all-to-all | bytes 4718592 | tf_op jit(solution)/shard_map/all_to_all | solution.py:24
  115.3 16.4 %collective-permute-start.1 = (bf16[4608,256]{1,0:T(8,128)(2,1)S(1)}, bf16[4608,256]{1,0:T(8,128)(2,1)}, u32[]{:S(2)}, u32[]{:S(2)}) collective-permute-start(bf16[4608,256]{1,0:T(8,128)(2,1)S(1)} %bitcast.58), channel_id=1, source_target_pairs={{0,1},{1,0},{2,3},{3,2},{4,5},{5,4},{6,7},{7,6},{8,9},{9,8},{10,11... | collective-permute-start | bytes 7077896 | tf_op jit(solution)/shard_map/ppermute | solution.py:239
  131.7 0.5 slice.53
  134.7 0.2 copy.33
  134.9 0.7 copy.34
  135.6 4.5 %all-to-all-start.5 = ((bf16[16,16,288]{2,1,0:T(8,128)(2,1)}), bf16[16,16,288]{2,1,0:T(8,128)(2,1)S(1)}, u32[]{:S(2)}, u32[]{:S(2)}) async-start(bf16[16,16,288]{2,1,0:T(8,128)(2,1)} %bitcast.16), calls=%async_computation.5 | async-start | bytes 393216 | tf_op jit(solution)/shard_map/all_to_all | solution.py:237
  140.1 3.6 %fusion.2 = f32[512,256]{1,0:T(8,128)} fusion(bf16[512,2304]{1,0:T(8,128)(2,1)} %bitcast.66, bf16[2304,768]{1,0:T(8,128)(2,1)} %all-gather.6.cloned.1.call-done), kind=kOutput, calls=%fused_computation.8 | convolution fusion | flops 603979776 | bytes 4063232 | tf_op jit(solution)/shard_map/dot_general | solution.py:212
  143.7 3.1 %all-to-all-done.5 = bf16[16,16,288]{2,1,0:T(8,128)(2,1)S(1)} async-done(((bf16[16,16,288]{2,1,0:T(8,128)(2,1)}), bf16[16,16,288]{2,1,0:T(8,128)(2,1)S(1)}, u32[]{:S(2)}, u32[]{:S(2)}) %all-to-all-start.5) | async-done | bytes 147488 | tf_op jit(solution)/shard_map/all_to_all | solution.py:237
  146.7 3.5 %all-to-all-start.3 = ((f32[2,256,256]{2,1,0:T(8,128)}), f32[2,256,256]{2,1,0:T(8,128)S(1)}, u32[]{:S(2)}, u32[]{:S(2)}) async-start(f32[2,256,256]{2,1,0:T(8,128)} %bitcast.70), calls=%async_computation.3 | async-start | bytes 1048576 | tf_op jit(solution)/shard_map/all_to_all | solution.py:221
  150.2 0.9 copy.41
  151.1 0.6 pad_add_fusion.where_ref
  151.7 0.7 copy.35
  152.4 1.1 reshape.114
  153.6 5.4 %all-to-all-done.3 = f32[2,256,256]{2,1,0:T(8,128)S(1)} async-done(((f32[2,256,256]{2,1,0:T(8,128)}), f32[2,256,256]{2,1,0:T(8,128)S(1)}, u32[]{:S(2)}, u32[]{:S(2)}) %all-to-all-start.3) | async-done | bytes 524320 | tf_op jit(solution)/shard_map/all_to_all | solution.py:221
  159.0 1.1 multiply_subtract_fusion.1
  160.1 0.1 fusion.7
  160.2 0.1 fusion.6
  160.3 0.7 pad_maximum_fusion.4.query_ref
  161.0 11.5 %all-gather.8.cloned.1.call-done.kv_hbm = bf16[8192,256]{1,0:T(8,128)(2,1)} async-done(((bf16[512,256]{1,0:T(8,128)(2,1)}), bf16[8192,256]{1,0:T(8,128)(2,1)}) %all-gather.8.cloned.1.call-update) | async-done | bytes 4194320 | tf_op jit(solution)/shard_map/all_gather | solution.py:218
  172.5 3.3 %shard_map.83 = (bf16[128,256]{1,0:T(8,128)(2,1)}, bf16[128,256]{1,0:T(8,128)(2,1)}) custom-call(s32[4]{0:T(128)} %pad_add_fusion.where_ref, bf16[512,128]{1,0:T(8,128)(2,1)} %pad_maximum_fusion.4.query_ref, s32[512,1]{1,0:T(8,128)} %bitcast.71, bf16[8192,256]{1,0:T(8,128)(2,1)} %all-gather.8.cloned.1.call-done.kv_hbm), custom_call_target="tpu_custom_call" | custom-call | flops 1073741824 | bytes 2097152 | tf_op jit(solution)/shard_map/pallas_call | solution.py:115
  175.9 11.3 %collective-permute-start.2 = (bf16[128,256]{1,0:T(8,128)(2,1)}, bf16[128,256]{1,0:T(8,128)(2,1)S(1)}, u32[]{:S(2)}, u32[]{:S(2)}) collective-permute-start(bf16[128,256]{1,0:T(8,128)(2,1)} %get-tuple-element.37), channel_id=1, source_target_pairs={{0,1},{1,0},{2,3},{3,2},{4,5},{5,4},{6,7},{7,6},{8,9},{9,8},{10,11... | collective-permute-start | bytes 196616 | tf_op jit(solution)/shard_map/ppermute | solution.py:245
  187.1 1.7 fusion.10
  188.9 2.6 %fusion.11 = f32[128,4608]{1,0:T(8,128)S(1)} fusion(bf16[128,256]{1,0:T(8,128)(2,1)S(1)} %collective-permute-done.2, bf16[4608,256]{1,0:T(8,128)(2,1)} %collective-permute-done.1), kind=kOutput, calls=%fused_computation.48 | convolution fusion | flops 301989888 | bytes 4784128 | tf_op jit(solution)/shard_map/dot_general | solution.py:248
  191.4 0.2 add_convert_fusion
  191.7 21.2 %all_to_all.42 = bf16[8,16,4608]{2,1,0:T(8,128)(2,1)S(1)} all-to-all(bf16[8,16,4608]{2,1,0:T(8,128)(2,1)S(1)} %bitcast.64), channel_id=1, replica_groups=mesh['xh'=2,'z'=16,'xl'=2,'y'=4,'c'=2] {'xl','y'}, dimensions={0} | all-to-all | bytes 2359296 | tf_op jit(solution)/shard_map/all_to_all | solution.py:255
  212.9 0.2 convert_reduce_fusion
  213.1 0.2 multiply_reduce_fusion.1
  213.2 0.1 add_convert_fusion.1
  213.4 0.1 broadcast_in_dim.84
  213.4 19.7 %all_to_all.43 = bf16[8,16,4608]{2,1,0:T(8,128)(2,1)S(1)} all-to-all(bf16[8,16,4608]{2,1,0:T(8,128)(2,1)S(1)} %broadcast_in_dim.84), channel_id=1, replica_groups=mesh['xh'=2,'z'=16,'xl'=2,'y'=4,'c'=2] {'xl','y'}, dimensions={0} | all-to-all | bytes 2359296 | tf_op jit(solution)/shard_map/all_to_all | solution.py:24
  233.2 3.8 %collective-permute-start.3 = (bf16[128,4608]{1,0:T(8,128)(2,1)S(1)}, bf16[128,4608]{1,0:T(8,128)(2,1)S(1)}, u32[]{:S(2)}, u32[]{:S(2)}) collective-permute-start(bf16[128,4608]{1,0:T(8,128)(2,1)S(1)} %bitcast.62), channel_id=1, source_target_pairs={{0,1},{1,0},{2,3},{3,2},{4,5},{5,4},{6,7},{7,6},{8,9},{9,8},{10,11... | collective-permute-start | bytes 3538952 | tf_op jit(solution)/shard_map/ppermute | solution.py:260
  237.1 2.4 collective-permute-done.3
  239.5 1.7 bitcast_select_fusion
  (35 shorter events, 0.4 us)
Async XLA Ops:
  6.5 75.9 %all-gather.6.cloned.1.call-start = ((), (), s32[]{:S(2)}) async-start(), calls=%async_computation.8 | async-start | bytes 3760128 | tf_op jit(solution)/shard_map/all_gather | solution.py:164
  6.5 17.1 %copy-start.5 = (f32[4608]{0:T(1024)S(1)}, f32[4608]{0:T(1024)}, u32[]{:S(2)}) copy-start(f32[4608]{0:T(1024)} %param.10) | copy-start | bytes 55300
  9.8 0.7 collective-permute-start
  11.6 29.0 %all-to-all-start = ((bf16[8,1,304,256]{3,2,1,0:T(8,128)(2,1)}), bf16[8,1,304,256]{3,2,1,0:T(8,128)(2,1)S(1)}, u32[]{:S(2)}, u32[]{:S(2)}) async-start(bf16[8,1,304,256]{3,2,1,0:T(8,128)(2,1)} %broadcast_in_dim.80), calls=%async_computation | async-start | bytes 2490368 | tf_op jit(solution)/shard_map/all_to_all | solution.py:24
  48.0 26.3 %all-to-all-start.2 = ((f32[16,1,8]{2,1,0:T(1,128)}), f32[16,1,8]{2,1,0:T(1,128)S(1)}, u32[]{:S(2)}, u32[]{:S(2)}) async-start(f32[16,1,8]{2,1,0:T(1,128)} %broadcast_in_dim.82), calls=%async_computation.2 | async-start | bytes 16384 | tf_op jit(solution)/shard_map/all_to_all | solution.py:24
  62.9 109.6 %all-gather.8.cloned.1.call-start = ((), (), s32[]{:S(2)}) async-start(), calls=%async_computation.9 | async-start | bytes 4456448 | tf_op jit(solution)/shard_map/all_gather | solution.py:218
  75.5 0.7 copy-start
  75.5 0.8 copy-start.2
  92.6 1.4 slice-start
  94.2 40.5 %copy-start.3 = (bf16[256,288]{0,1:T(8,128)(2,1)S(1)}, bf16[256,288]{0,1:T(8,128)(2,1)}, u32[]{:S(2)}) copy-start(bf16[256,288]{0,1:T(8,128)(2,1)} %param.8) | copy-start | bytes 442372
  115.3 45.7 %collective-permute-start.1 = (bf16[4608,256]{1,0:T(8,128)(2,1)S(1)}, bf16[4608,256]{1,0:T(8,128)(2,1)}, u32[]{:S(2)}, u32[]{:S(2)}) collective-permute-start(bf16[4608,256]{1,0:T(8,128)(2,1)S(1)} %bitcast.58), channel_id=1, source_target_pairs={{0,1},{1,0},{2,3},{3,2},{4,5},{5,4},{6,7},{7,6},{8,9},{9,8},{10,11... | collective-permute-start | bytes 7077896 | tf_op jit(solution)/shard_map/ppermute | solution.py:239
  135.6 11.1 %all-to-all-start.5 = ((bf16[16,16,288]{2,1,0:T(8,128)(2,1)}), bf16[16,16,288]{2,1,0:T(8,128)(2,1)S(1)}, u32[]{:S(2)}, u32[]{:S(2)}) async-start(bf16[16,16,288]{2,1,0:T(8,128)(2,1)} %bitcast.16), calls=%async_computation.5 | async-start | bytes 393216 | tf_op jit(solution)/shard_map/all_to_all | solution.py:237
  143.7 15.4 %copy-start.1 = (f32[512,64]{1,0:T(8,128)S(1)}, f32[512,64]{1,0:T(8,128)}, u32[]{:S(2)}) copy-start(f32[512,64]{1,0:T(8,128)} %copy-done) | copy-start | bytes 393220
  146.7 12.3 %all-to-all-start.3 = ((f32[2,256,256]{2,1,0:T(8,128)}), f32[2,256,256]{2,1,0:T(8,128)S(1)}, u32[]{:S(2)}, u32[]{:S(2)}) async-start(f32[2,256,256]{2,1,0:T(8,128)} %bitcast.70), calls=%async_computation.3 | async-start | bytes 1048576 | tf_op jit(solution)/shard_map/all_to_all | solution.py:221
  175.9 13.0 %collective-permute-start.2 = (bf16[128,256]{1,0:T(8,128)(2,1)}, bf16[128,256]{1,0:T(8,128)(2,1)S(1)}, u32[]{:S(2)}, u32[]{:S(2)}) collective-permute-start(bf16[128,256]{1,0:T(8,128)(2,1)} %get-tuple-element.37), channel_id=1, source_target_pairs={{0,1},{1,0},{2,3},{3,2},{4,5},{5,4},{6,7},{7,6},{8,9},{9,8},{10,11... | collective-permute-start | bytes 196616 | tf_op jit(solution)/shard_map/ppermute | solution.py:245
  191.7 21.6 %copy-start.4 = (f32[4608]{0:T(1024)S(1)}, f32[4608]{0:T(1024)}, u32[]{:S(2)}) copy-start(f32[4608]{0:T(1024)} %param.11) | copy-start | bytes 55300
  233.2 6.3 %collective-permute-start.3 = (bf16[128,4608]{1,0:T(8,128)(2,1)S(1)}, bf16[128,4608]{1,0:T(8,128)(2,1)S(1)}, u32[]{:S(2)}, u32[]{:S(2)}) collective-permute-start(bf16[128,4608]{1,0:T(8,128)(2,1)S(1)} %bitcast.62), channel_id=1, source_target_pairs={{0,1},{1,0},{2,3},{3,2},{4,5},{5,4},{6,7},{7,6},{8,9},{9,8},{10,11... | collective-permute-start | bytes 3538952 | tf_op jit(solution)/shard_map/ppermute | solution.py:260
Sparse Core Ops, SparseCore 0:
  9.4 73.0 all-gather.5
  93.6 78.8 all-gather.7

commit v2 on v0

--- a/solution.py
+++ b/solution.py
@@ -155,6 +155,41 @@
         out_specs=vmem,
         compiler_params=pltpu.CompilerParams(vmem_limit_bytes=16 * 1024 * 1024),
     )(side, part, both, cosine, sine)
+
+
+def far_kernel(far_ref, near_ref, weight_hbm, out_ref, held, sem):
+    pieces, width = held.shape[:2]
+
+    def fetch(k):
+        return pltpu.make_async_copy(
+            weight_hbm.at[pl.ds(k * width, width), :], held.at[k], sem.at[k]
+        )
+
+    for k in range(pieces):
+        fetch(k).start()
+    for k in range(pieces):
+        fetch(k).wait()
+        columns = slice(k * width, (k + 1) * width)
+        product = lax.dot_general(
+            far_ref[...], held[k], (((1,), (1,)), ((), ())), preferred_element_type=jnp.float32
+        )
+        out_ref[:, columns] = (near_ref[:, columns] + product).astype(jnp.bfloat16)
+
+
+def add_far(far, near_part, rows_of):
+    pieces = 6
+    vmem = pl.BlockSpec(memory_space=pltpu.VMEM)
+    return pl.pallas_call(
+        far_kernel,
+        out_shape=jax.ShapeDtypeStruct(near_part.shape, jnp.bfloat16),
+        in_specs=[vmem, vmem, pl.BlockSpec(memory_space=pltpu.HBM)],
+        out_specs=vmem,
+        scratch_shapes=[
+            pltpu.VMEM((pieces, rows_of.shape[0] // pieces, rows_of.shape[1]), jnp.bfloat16),
+            pltpu.SemaphoreType.DMA((pieces,)),
+        ],
+        compiler_params=pltpu.CompilerParams(vmem_limit_bytes=16 * 1024 * 1024),
+    )(far, near_part, rows_of)
 
 
 def local(tokens, segments, pre_gain, post_gain, w_query, w_key, w_value, w_out):
@@ -249,7 +284,7 @@
 
     near_part = through(kept, out_t)
     near_part, far = lax.optimization_barrier((near_part, far))
-    halves = (near_part + through(far, out_far)).astype(jnp.bfloat16)
+    halves = add_far(far, near_part, out_far)
     pieces = lax.all_to_all(halves.reshape(near, few, D), PLANE, 0, 0, tiled=True)
     proj = jnp.sum(pieces.astype(jnp.float32), axis=0)
     post = lax.rsqrt(jnp.mean(proj * proj, axis=1, keepdims=True) + EPS)

time: 250 us -> 250 us (level)
  Pallas kernels: 4.21 us -> 7.2 us
    pallas_call x0 -> x1, Pallas kernels: none -> 2.99 us  [add_far(): pl.pallas_call(far_kernel, out_shape=jax.ShapeDtypeStruct(near_part.shape...]
where the time goes in v2:
time: 250 us; the launch traced here: 247 us
  blocking collectives  97.9 us (39%)
  starting transfers between devices  50.6 us (20%)
  waiting for transfers between devices  45.6 us (18%)
  between operations  16.3 us (7%)
  other arithmetic  11.3 us (5%)
  local copies, waits for them, and re-layouts  9.62 us (4%)
  matrix products  8.96 us (4%)
  Pallas kernels  7.2 us (3%)
    all_to_all x3, blocking collectives, from_everyone(): return lax.all_to_all(copies, axis, split_axis=0, concat_axis=0, tiled=True)  48.6 us
    all_to_all x1, blocking collectives, local(): lax.all_to_all(halves.reshape(near, few, D), PLANE, 0, 0, tiled=True)  21.1 us
    all_to_all x2, starting transfers between devices, from_everyone(): return lax.all_to_all(copies, axis, split_axis=0, concat_axis=0, tiled=True)  18.5 us
    all_to_all x2, waiting for transfers between devices, from_everyone(): return lax.all_to_all(copies, axis, split_axis=0, concat_axis=0, tiled=True)  18.3 us
    all_gather x1, waiting for transfers between devices, local(): kv_all = lax.all_gather(kv_pair, 'z', axis=0, tiled=True)  16.9 us
    all_to_all x1, blocking collectives, local(): lax.all_to_all(pieces, HEAD, 0, 0, tiled=True).transpose(1, 0, 2)  16.1 us
    ppermute x1, starting transfers between devices, local(): out_far = lax.ppermute(out_t, 'c', swap)  12.7 us
    ppermute x1, starting transfers between devices, local(): far = lax.ppermute(away, 'c', swap)  11.4 us
  transfers between devices with their start and end apart: 9, of which 5 were waited for; matrix products, arithmetic and copies ran while one was open for 9% of the time, Pallas kernels for 0%

profile of v2, /device:TPU:1, one launch (start us, length us, event | category | flops | bytes accessed | tf_op | source)
XLA Modules:
  0.0 247.5 jit_solution(1277704717717070645)
XLA Ops:
  6.5 1.6 pad_maximum_fusion.2
  8.2 0.0 all-gather.6.cloned.1.call-update
  8.2 0.7 convert_element_type.68
  8.9 0.9 pad_maximum_fusion.3
  9.8 0.7 collective-permute-start
  10.5 1.1 copy.33
  11.6 16.1 %all_to_all.40 = bf16[16,16,288]{2,1,0:T(8,128)(2,1)S(1)} all-to-all(bf16[16,16,288]{2,1,0:T(8,128)(2,1)S(1)} %bitcast.64), channel_id=1, replica_groups=mesh['xh'=2,'z'=16,'xl'=2,'y'=4,'c'=2] {'xl','y','c'}, dimensions={0} | all-to-all | bytes 294912 | tf_op jit(solution)/shard_map/all_to_all | solution.py:243
  27.7 1.1 broadcast_in_dim.79
  28.8 3.6 %all-to-all-start = ((bf16[8,1,304,256]{3,2,1,0:T(8,128)(2,1)}), bf16[8,1,304,256]{3,2,1,0:T(8,128)(2,1)S(1)}, u32[]{:S(2)}, u32[]{:S(2)}) async-start(bf16[8,1,304,256]{3,2,1,0:T(8,128)(2,1)} %broadcast_in_dim.79), calls=%async_computation | async-start | bytes 2490368 | tf_op jit(solution)/shard_map/all_to_all | solution.py:24
  32.4 0.1 dynamic_slice.13
  32.6 0.9 reshape.112
  33.4 16.1 %all-to-all-done = bf16[8,1,304,256]{3,2,1,0:T(8,128)(2,1)S(1)} async-done(((bf16[8,1,304,256]{3,2,1,0:T(8,128)(2,1)}), bf16[8,1,304,256]{3,2,1,0:T(8,128)(2,1)S(1)}, u32[]{:S(2)}, u32[]{:S(2)}) %all-to-all-start) | async-done | bytes 1245216 | tf_op jit(solution)/shard_map/all_to_all | solution.py:24
  49.5 0.2 broadcast_in_dim.80
  49.7 6.0 %all_to_all.41 = bf16[2,1,8,304,256]{4,3,2,1,0:T(8,128)(2,1)S(1)} all-to-all(bf16[2,1,8,304,256]{4,3,2,1,0:T(8,128)(2,1)S(1)} %broadcast_in_dim.80), channel_id=1, replica_groups=mesh['xh'=2,'z'=16,'xl'=2,'y'=4,'c'=2] {'c'}, dimensions={0} | all-to-all | bytes 4980736 | tf_op jit(solution)/shard_map/all_to_all | solution.py:24
  55.7 0.2 copy.30
  55.9 0.1 convert_reduce_fusion.1
  56.0 0.6 broadcast_in_dim.81
  56.6 14.9 %all-to-all-start.2 = ((f32[16,1,8]{2,1,0:T(1,128)}), f32[16,1,8]{2,1,0:T(1,128)S(1)}, u32[]{:S(2)}, u32[]{:S(2)}) async-start(f32[16,1,8]{2,1,0:T(1,128)} %broadcast_in_dim.81), calls=%async_computation.2 | async-start | bytes 16384 | tf_op jit(solution)/shard_map/all_to_all | solution.py:24
  71.5 0.0 all-gather.8.cloned.1.call-start
  71.6 0.5 multiply_reduce_fusion
  72.1 4.7 %all-gather.2 = f32[2,2,256]{2,1,0:T(2,128)S(1)} all-gather(f32[1,2,256]{2,1,0:T(2,128)S(1)} %bitcast.74), channel_id=2, replica_groups=mesh['xh'=2,'z'=16,'xl'=2,'y'=4,'c'=2] {'xh'}, dimensions={0}, use_global_device_ids=true | all-gather | bytes 6144 | tf_op jit(solution)/shard_map/all_gather | solution.py:235
  76.8 0.5 slice_convert_fusion
  77.3 0.8 fusion.1
  78.1 2.4 copy.31
  80.6 2.2 all-to-all-done.2
  82.8 0.1 select_reduce_fusion
  82.9 0.1 subtract_bitcast_fusion
  83.0 1.0 fusion.8
  84.0 0.7 copy-done
  84.7 0.1 copy-done.2
  84.8 0.2 pad_maximum_fusion
  85.0 0.0 all-gather.6.cloned.1.call-done
  85.0 2.8 %fusion.9 = (bf16[512,256]{1,0:T(8,128)(2,1)S(1)}, f32[512,256]{1,0:T(8,128)S(1)}) fusion(bf16[512,2304]{1,0:T(8,128)(2,1)} %bitcast.61, bf16[2304,768]{1,0:T(8,128)(2,1)} %all-gather.6.cloned.1.call-done), kind=kOutput, calls=%fused_computation.45 | convolution fusion | flops 604110848 | bytes 4325376 | tf_op jit(solution)/shard_map/dot_general | solution.py:251
  87.8 7.4 %all-gather.1 = bf16[1024,256]{1,0:T(8,128)(2,1)S(1)} all-gather(bf16[512,256]{1,0:T(8,128)(2,1)S(1)} %get-tuple-element.46), channel_id=3, replica_groups=mesh['xh'=2,'z'=16,'xl'=2,'y'=4,'c'=2] {'xh'}, dimensions={0}, use_global_device_ids=true | all-gather | bytes 786432 | tf_op jit(solution)/shard_map/all_gather | solution.py:254
  95.2 0.8 shard_map.82
  96.1 0.5 slice-done
  96.5 0.2 broadcast_in_dim.83
  96.7 22.8 %all_to_all.42 = bf16[2,1,2304,256]{3,2,1,0:T(8,128)(2,1)} all-to-all(bf16[2,1,2304,256]{3,2,1,0:T(8,128)(2,1)S(1)} %broadcast_in_dim.83), channel_id=1, replica_groups=mesh['xh'=2,'z'=16,'xl'=2,'y'=4,'c'=2] {'xh'}, dimensions={0} | all-to-all | bytes 4718592 | tf_op jit(solution)/shard_map/all_to_all | solution.py:24
  119.5 12.7 %collective-permute-start.1 = (bf16[4608,256]{1,0:T(8,128)(2,1)}, bf16[4608,256]{1,0:T(8,128)(2,1)S(1)}, u32[]{:S(2)}, u32[]{:S(2)}) collective-permute-start(bf16[4608,256]{1,0:T(8,128)(2,1)} %bitcast.21), channel_id=1, source_target_pairs={{0,1},{1,0},{2,3},{3,2},{4,5},{5,4},{6,7},{7,6},{8,9},{9,8},{10,11... | collective-permute-start | bytes 7077896 | tf_op jit(solution)/shard_map/ppermute | solution.py:274
  132.3 0.6 slice.49
  135.4 3.6 %fusion.2 = f32[512,256]{1,0:T(8,128)} fusion(bf16[512,2304]{1,0:T(8,128)(2,1)} %bitcast.62, bf16[2304,768]{1,0:T(8,128)(2,1)} %all-gather.6.cloned.1.call-done), kind=kOutput, calls=%fused_computation.7 | convolution fusion | flops 603979776 | bytes 4063232 | tf_op jit(solution)/shard_map/dot_general | solution.py:251
  139.0 3.5 %all-to-all-start.4 = ((f32[2,256,256]{2,1,0:T(8,128)}), f32[2,256,256]{2,1,0:T(8,128)S(1)}, u32[]{:S(2)}, u32[]{:S(2)}) async-start(f32[2,256,256]{2,1,0:T(8,128)} %bitcast.67), calls=%async_computation.4 | async-start | bytes 1048576 | tf_op jit(solution)/shard_map/all_to_all | solution.py:260
  142.5 0.9 copy.41
  143.4 0.6 pad_add_fusion.where_ref
  144.0 8.0 %all-to-all-done.4 = f32[2,256,256]{2,1,0:T(8,128)S(1)} async-done(((f32[2,256,256]{2,1,0:T(8,128)}), f32[2,256,256]{2,1,0:T(8,128)S(1)}, u32[]{:S(2)}, u32[]{:S(2)}) %all-to-all-start.4) | async-done | bytes 524320 | tf_op jit(solution)/shard_map/all_to_all | solution.py:260
  152.1 1.0 multiply_subtract_fusion.1
  153.1 0.1 fusion.7
  153.2 0.1 fusion.6
  153.3 0.7 pad_maximum_fusion.4.query_ref
  154.0 16.9 %all-gather.8.cloned.1.call-done.kv_hbm = bf16[8192,256]{1,0:T(8,128)(2,1)} async-done(((bf16[512,256]{1,0:T(8,128)(2,1)}), bf16[8192,256]{1,0:T(8,128)(2,1)}) %all-gather.8.cloned.1.call-update) | async-done | bytes 4194320 | tf_op jit(solution)/shard_map/all_gather | solution.py:257
  170.9 3.4 %shard_map.83 = (bf16[128,256]{1,0:T(8,128)(2,1)}, bf16[128,256]{1,0:T(8,128)(2,1)}) custom-call(s32[4]{0:T(128)} %pad_add_fusion.where_ref, bf16[512,128]{1,0:T(8,128)(2,1)} %pad_maximum_fusion.4.query_ref, s32[512,1]{1,0:T(8,128)} %bitcast.68, bf16[8192,256]{1,0:T(8,128)(2,1)} %all-gather.8.cloned.1.call-done.kv_hbm), custom_call_target="tpu_custom_call" | custom-call | flops 1073741824 | bytes 2097152 | tf_op jit(solution)/shard_map/pallas_call | solution.py:115
  174.2 11.4 %collective-permute-start.2 = (bf16[128,256]{1,0:T(8,128)(2,1)}, bf16[128,256]{1,0:T(8,128)(2,1)S(1)}, u32[]{:S(2)}, u32[]{:S(2)}) collective-permute-start(bf16[128,256]{1,0:T(8,128)(2,1)} %get-tuple-element.35), channel_id=1, source_target_pairs={{0,1},{1,0},{2,3},{3,2},{4,5},{5,4},{6,7},{7,6},{8,9},{9,8},{10,11... | collective-permute-start | bytes 196616 | tf_op jit(solution)/shard_map/ppermute | solution.py:278
  185.6 2.6 %fusion.10.near_ref = f32[128,4608]{1,0:T(8,128)S(1)} fusion(bf16[128,256]{1,0:T(8,128)(2,1)} %get-tuple-element.33, bf16[4608,256]{1,0:T(8,128)(2,1)} %bitcast.21), kind=kOutput, calls=%fused_computation.46 | convolution fusion | flops 301989888 | bytes 4784128 | tf_op jit(solution)/shard_map/dot_general | solution.py:281
  188.2 3.0 %shard_map.84 = bf16[128,4608]{1,0:T(8,128)(2,1)S(1)} custom-call(bf16[128,256]{1,0:T(8,128)(2,1)S(1)} %collective-permute-done.2.far_ref, f32[128,4608]{1,0:T(8,128)S(1)} %fusion.10.near_ref, bf16[4608,256]{1,0:T(8,128)(2,1)S(1)} %collective-permute-done.1.weight_hbm), custom_call_target="tpu_custom_call" | custom-call | tf_op jit(solution)/shard_map/pallas_call | solution.py:182
  191.3 21.1 %all_to_all.43 = bf16[8,16,4608]{2,1,0:T(8,128)(2,1)S(1)} all-to-all(bf16[8,16,4608]{2,1,0:T(8,128)(2,1)S(1)} %bitcast.52), channel_id=1, replica_groups=mesh['xh'=2,'z'=16,'xl'=2,'y'=4,'c'=2] {'xl','y'}, dimensions={0} | all-to-all | bytes 2359296 | tf_op jit(solution)/shard_map/all_to_all | solution.py:288
  212.3 0.2 convert_reduce_fusion
  212.5 0.2 multiply_reduce_fusion.1
  212.7 0.1 add_convert_fusion
  212.8 0.1 broadcast_in_dim.84
  212.9 19.7 %all_to_all.44 = bf16[8,16,4608]{2,1,0:T(8,128)(2,1)S(1)} all-to-all(bf16[8,16,4608]{2,1,0:T(8,128)(2,1)S(1)} %broadcast_in_dim.84), channel_id=1, replica_groups=mesh['xh'=2,'z'=16,'xl'=2,'y'=4,'c'=2] {'xl','y'}, dimensions={0} | all-to-all | bytes 2359296 | tf_op jit(solution)/shard_map/all_to_all | solution.py:24
  232.6 3.8 %collective-permute-start.3 = (bf16[128,4608]{1,0:T(8,128)(2,1)S(1)}, bf16[128,4608]{1,0:T(8,128)(2,1)S(1)}, u32[]{:S(2)}, u32[]{:S(2)}) collective-permute-start(bf16[128,4608]{1,0:T(8,128)(2,1)S(1)} %bitcast.59), channel_id=1, source_target_pairs={{0,1},{1,0},{2,3},{3,2},{4,5},{5,4},{6,7},{7,6},{8,9},{9,8},{10,11... | collective-permute-start | bytes 3538952 | tf_op jit(solution)/shard_map/ppermute | solution.py:293
  236.5 0.1 broadcast_bitcast_fusion.1
  236.6 2.4 collective-permute-done.3
  238.9 1.7 bitcast_select_fusion
  (33 shorter events, 0.3 us)
Async XLA Ops:
  6.5 78.5 %all-gather.6.cloned.1.call-start = ((), (), s32[]{:S(2)}) async-start(), calls=%async_computation.8 | async-start | bytes 3760128 | tf_op jit(solution)/shard_map/all_gather | solution.py:199
  9.8 17.9 %collective-permute-start = (bf16[304,256]{1,0:T(8,128)(2,1)S(1)}, bf16[304,256]{1,0:T(8,128)(2,1)S(1)}, u32[]{:S(2)}, u32[]{:S(2)}) collective-permute-start(bf16[304,256]{1,0:T(8,128)(2,1)S(1)} %pad_maximum_fusion.3), channel_id=1, source_target_pairs={{0,0},{8,256},{256,8},{264,264},{1,1},{9,257},{257,9},{265,265},{2... | collective-permute-start | bytes 466952 | tf_op jit(solution)/shard_map/ppermute | solution.py:204
  11.6 20.8 %copy-start.5 = (f32[4608]{0:T(1024)S(1)}, f32[4608]{0:T(1024)}, u32[]{:S(2)}) copy-start(f32[4608]{0:T(1024)} %param.10) | copy-start | bytes 55300
  28.8 20.7 %all-to-all-start = ((bf16[8,1,304,256]{3,2,1,0:T(8,128)(2,1)}), bf16[8,1,304,256]{3,2,1,0:T(8,128)(2,1)S(1)}, u32[]{:S(2)}, u32[]{:S(2)}) async-start(bf16[8,1,304,256]{3,2,1,0:T(8,128)(2,1)} %broadcast_in_dim.79), calls=%async_computation | async-start | bytes 2490368 | tf_op jit(solution)/shard_map/all_to_all | solution.py:24
  56.6 26.2 %all-to-all-start.2 = ((f32[16,1,8]{2,1,0:T(1,128)}), f32[16,1,8]{2,1,0:T(1,128)S(1)}, u32[]{:S(2)}, u32[]{:S(2)}) async-start(f32[16,1,8]{2,1,0:T(1,128)} %broadcast_in_dim.81), calls=%async_computation.2 | async-start | bytes 16384 | tf_op jit(solution)/shard_map/all_to_all | solution.py:24
  71.5 99.4 %all-gather.8.cloned.1.call-start = ((), (), s32[]{:S(2)}) async-start(), calls=%async_computation.9 | async-start | bytes 4456448 | tf_op jit(solution)/shard_map/all_gather | solution.py:257
  84.0 0.7 copy-start
  84.0 0.8 copy-start.2
  95.2 1.4 slice-start
  119.5 34.5 %collective-permute-start.1 = (bf16[4608,256]{1,0:T(8,128)(2,1)}, bf16[4608,256]{1,0:T(8,128)(2,1)S(1)}, u32[]{:S(2)}, u32[]{:S(2)}) collective-permute-start(bf16[4608,256]{1,0:T(8,128)(2,1)} %bitcast.21), channel_id=1, source_target_pairs={{0,1},{1,0},{2,3},{3,2},{4,5},{5,4},{6,7},{7,6},{8,9},{9,8},{10,11... | collective-permute-start | bytes 7077896 | tf_op jit(solution)/shard_map/ppermute | solution.py:274
  135.4 16.7 %copy-start.1 = (f32[512,64]{1,0:T(8,128)S(1)}, f32[512,64]{1,0:T(8,128)}, u32[]{:S(2)}) copy-start(f32[512,64]{1,0:T(8,128)} %copy-done) | copy-start | bytes 393220
  139.0 13.0 %all-to-all-start.4 = ((f32[2,256,256]{2,1,0:T(8,128)}), f32[2,256,256]{2,1,0:T(8,128)S(1)}, u32[]{:S(2)}, u32[]{:S(2)}) async-start(f32[2,256,256]{2,1,0:T(8,128)} %bitcast.67), calls=%async_computation.4 | async-start | bytes 1048576 | tf_op jit(solution)/shard_map/all_to_all | solution.py:260
  174.2 14.0 %collective-permute-start.2 = (bf16[128,256]{1,0:T(8,128)(2,1)}, bf16[128,256]{1,0:T(8,128)(2,1)S(1)}, u32[]{:S(2)}, u32[]{:S(2)}) collective-permute-start(bf16[128,256]{1,0:T(8,128)(2,1)} %get-tuple-element.35), channel_id=1, source_target_pairs={{0,1},{1,0},{2,3},{3,2},{4,5},{5,4},{6,7},{7,6},{8,9},{9,8},{10,11... | collective-permute-start | bytes 196616 | tf_op jit(solution)/shard_map/ppermute | solution.py:278
  191.2 21.4 %copy-start.3 = (bf16[16,4608]{1,0:T(8,128)(2,1)S(1)}, bf16[16,4608]{1,0:T(8,128)(2,1)}, u32[]{:S(2)}) copy-start(bf16[16,4608]{1,0:T(8,128)(2,1)} %reshape.112) | copy-start | bytes 442372
  191.2 21.4 %copy-start.4 = (f32[4608]{0:T(1024)S(1)}, f32[4608]{0:T(1024)}, u32[]{:S(2)}) copy-start(f32[4608]{0:T(1024)} %param.11) | copy-start | bytes 55300
  232.6 6.3 %collective-permute-start.3 = (bf16[128,4608]{1,0:T(8,128)(2,1)S(1)}, bf16[128,4608]{1,0:T(8,128)(2,1)S(1)}, u32[]{:S(2)}, u32[]{:S(2)}) collective-permute-start(bf16[128,4608]{1,0:T(8,128)(2,1)S(1)} %bitcast.59), channel_id=1, source_target_pairs={{0,1},{1,0},{2,3},{3,2},{4,5},{5,4},{6,7},{7,6},{8,9},{9,8},{10,11... | collective-permute-start | bytes 3538952 | tf_op jit(solution)/shard_map/ppermute | solution.py:293
Sparse Core Ops, SparseCore 0:
  9.4 73.2 all-gather.5
  96.2 74.6 all-gather.7

commit v3 on v0

--- a/solution.py
+++ b/solution.py
@@ -54,29 +54,27 @@
     sums[...] = jnp.zeros_like(sums)
     total[...] = jnp.zeros_like(total)
 
-    def gather(j, count, masked):
+    def weigh(keys):
+        scores = lax.dot_general(
+            query_ref[...], keys, (((1,), (1,)), ((), ())), preferred_element_type=jnp.float32
+        )
+        return jnp.exp(CAP * jnp.tanh(scores * (1.0 / CAP)))
+
+    def add(weights, values):
+        part = weights[:, :HD]
+        for k in range(1, weights.shape[1] // HD):
+            part = part + weights[:, k * HD : (k + 1) * HD]
+        sums[...] += part
+        total[...] += jnp.dot(
+            weights.astype(jnp.bfloat16), values, preferred_element_type=jnp.float32
+        )
+
+    def gather(j, count):
         for k in range(count):
             fetch(j + k).wait()
         keys = held[pl.ds(j, count), :, :HD].reshape(count * rows, HD)
         values = held[pl.ds(j, count), :, HD:].reshape(count * rows, HD)
-        scores = lax.dot_general(
-            query_ref[...], keys, (((1,), (1,)), ((), ())), preferred_element_type=jnp.float32
-        )
-        weights = jnp.exp(CAP * jnp.tanh(scores * (1.0 / CAP)))
-        if masked:
-            shape = (GROUP * rows, rows)
-            row = lax.broadcasted_iota(jnp.int32, shape, 0)
-            index = own * rows + jnp.where(row >= rows, row - rows, row)
-            key_index = j * rows + lax.broadcasted_iota(jnp.int32, shape, 1)
-            allowed = (key_index >= start_ref[...]) & (key_index <= index)
-            weights = jnp.where(allowed, weights, 0.0)
-        part = weights[:, :HD]
-        for k in range(1, count * rows // HD):
-            part = part + weights[:, k * HD : (k + 1) * HD]
-        sums[...] += part
-        total[...] += jnp.dot(
-            weights.astype(jnp.bfloat16), values, preferred_element_type=jnp.float32
-        )
+        add(weigh(keys), values)
 
     done = low + 1
     for count in (4, 2, 1):
@@ -84,7 +82,7 @@
 
         @pl.loop(0, steps)
         def _(i, done=done, count=count):
-            gather(done + i * count, count, False)
+            gather(done + i * count, count)
 
         done = done + steps * count
 
@@ -94,9 +92,22 @@
 
     @pl.when(low < own)
     def _():
-        gather(low, 1, True)
-
-    gather(own, 1, True)
+        fetch(low).wait()
+
+    fetch(own).wait()
+    weights = weigh(jnp.concatenate([held[low, :, :HD], held[own, :, :HD]], axis=0))
+    shape = (GROUP * rows, rows)
+    row = lax.broadcasted_iota(jnp.int32, shape, 0)
+    row = jnp.where(row >= rows, row - rows, row)
+    column = lax.broadcasted_iota(jnp.int32, shape, 1)
+    edge = jnp.where(low < own, low * rows, -rows)
+    early = jnp.where(edge + column >= start_ref[...], weights[:, :rows], 0.0)
+    late = (own * rows + column >= start_ref[...]) & (column <= row)
+    late = jnp.where(late, weights[:, rows:], 0.0)
+    add(
+        jnp.concatenate([early, late], axis=1),
+        jnp.concatenate([held[low, :, HD:], held[own, :, HD:]], axis=0),
+    )
 
     result = total[...] / jnp.sum(sums[...], axis=1, keepdims=True)
     south = where_ref[3] == 0

time: 250 us -> 249 us (level)
  no operation moved by 1% of the time
where the time goes in v3:
time: 249 us; the launch traced here: 248 us
  blocking collectives  96.1 us (39%)
  starting transfers between devices  51.3 us (21%)
  waiting for transfers between devices  47.7 us (19%)
  between operations  16.3 us (7%)
  other arithmetic  11.5 us (5%)
  matrix products  10.7 us (4%)
  local copies, waits for them, and re-layouts  9.62 us (4%)
  Pallas kernels  4.33 us (2%)
    all_to_all x3, blocking collectives, from_everyone(): return lax.all_to_all(copies, axis, split_axis=0, concat_axis=0, tiled=True)  46.5 us
    all_to_all x1, blocking collectives, local(): lax.all_to_all(halves.reshape(near, few, D), PLANE, 0, 0, tiled=True)  21.4 us
    all_gather x1, waiting for transfers between devices, local(): kv_all = lax.all_gather(kv_pair, 'z', axis=0, tiled=True)  19 us
    all_to_all x2, starting transfers between devices, from_everyone(): return lax.all_to_all(copies, axis, split_axis=0, concat_axis=0, tiled=True)  18.5 us
    all_to_all x2, waiting for transfers between devices, from_everyone(): return lax.all_to_all(copies, axis, split_axis=0, concat_axis=0, tiled=True)  18.3 us
    all_to_all x1, blocking collectives, local(): lax.all_to_all(pieces, HEAD, 0, 0, tiled=True).transpose(1, 0, 2)  16.1 us
    ppermute x1, starting transfers between devices, local(): out_far = lax.ppermute(out_t, 'c', swap)  13.8 us
    ppermute x1, starting transfers between devices, local(): far = lax.ppermute(away, 'c', swap)  11 us
  transfers between devices with their start and end apart: 9, of which 5 were waited for; matrix products, arithmetic and copies ran while one was open for 9% of the time, Pallas kernels for 0%

profile of v3, /device:TPU:1, one launch (start us, length us, event | category | flops | bytes accessed | tf_op | source)
XLA Modules:
  0.0 247.5 jit_solution(13681604119965849838)
XLA Ops:
  6.5 1.6 pad_maximum_fusion.2
  8.2 0.7 convert_element_type.71
  8.9 0.9 pad_maximum_fusion.3
  9.8 0.7 collective-permute-start
  10.5 1.1 copy.33
  11.6 16.1 %all_to_all.40 = bf16[16,16,288]{2,1,0:T(8,128)(2,1)S(1)} all-to-all(bf16[16,16,288]{2,1,0:T(8,128)(2,1)S(1)} %bitcast.68), channel_id=1, replica_groups=mesh['xh'=2,'z'=16,'xl'=2,'y'=4,'c'=2] {'xl','y','c'}, dimensions={0} | all-to-all | bytes 294912 | tf_op jit(solution)/shard_map/all_to_all | solution.py:219
  27.7 1.1 broadcast_in_dim.79
  28.8 3.6 %all-to-all-start = ((bf16[8,1,304,256]{3,2,1,0:T(8,128)(2,1)}), bf16[8,1,304,256]{3,2,1,0:T(8,128)(2,1)S(1)}, u32[]{:S(2)}, u32[]{:S(2)}) async-start(bf16[8,1,304,256]{3,2,1,0:T(8,128)(2,1)} %broadcast_in_dim.79), calls=%async_computation | async-start | bytes 2490368 | tf_op jit(solution)/shard_map/all_to_all | solution.py:24
  32.4 0.1 dynamic_slice.13
  32.6 0.9 reshape.112
  33.4 16.1 %all-to-all-done = bf16[8,1,304,256]{3,2,1,0:T(8,128)(2,1)S(1)} async-done(((bf16[8,1,304,256]{3,2,1,0:T(8,128)(2,1)}), bf16[8,1,304,256]{3,2,1,0:T(8,128)(2,1)S(1)}, u32[]{:S(2)}, u32[]{:S(2)}) %all-to-all-start) | async-done | bytes 1245216 | tf_op jit(solution)/shard_map/all_to_all | solution.py:24
  49.5 0.2 broadcast_in_dim.80
  49.7 6.0 %all_to_all.41 = bf16[2,1,8,304,256]{4,3,2,1,0:T(8,128)(2,1)S(1)} all-to-all(bf16[2,1,8,304,256]{4,3,2,1,0:T(8,128)(2,1)S(1)} %broadcast_in_dim.80), channel_id=1, replica_groups=mesh['xh'=2,'z'=16,'xl'=2,'y'=4,'c'=2] {'c'}, dimensions={0} | all-to-all | bytes 4980736 | tf_op jit(solution)/shard_map/all_to_all | solution.py:24
  55.7 0.2 copy.30
  55.9 0.1 convert_reduce_fusion.1
  56.0 0.6 broadcast_in_dim.81
  56.6 14.9 %all-to-all-start.2 = ((f32[16,1,8]{2,1,0:T(1,128)}), f32[16,1,8]{2,1,0:T(1,128)S(1)}, u32[]{:S(2)}, u32[]{:S(2)}) async-start(f32[16,1,8]{2,1,0:T(1,128)} %broadcast_in_dim.81), calls=%async_computation.2 | async-start | bytes 16384 | tf_op jit(solution)/shard_map/all_to_all | solution.py:24
  71.5 0.0 all-gather.8.cloned.1.call-start
  71.6 0.5 multiply_reduce_fusion
  72.1 4.7 %all-gather.2 = f32[2,2,256]{2,1,0:T(2,128)S(1)} all-gather(f32[1,2,256]{2,1,0:T(2,128)S(1)} %bitcast.78), channel_id=2, replica_groups=mesh['xh'=2,'z'=16,'xl'=2,'y'=4,'c'=2] {'xh'}, dimensions={0}, use_global_device_ids=true | all-gather | bytes 6144 | tf_op jit(solution)/shard_map/all_gather | solution.py:211
  76.8 0.5 slice_convert_fusion
  77.3 0.8 fusion.1
  78.1 2.4 copy.31
  80.6 2.2 all-to-all-done.2
  82.8 0.1 select_reduce_fusion
  82.9 0.1 subtract_bitcast_fusion
  83.0 1.0 fusion.8
  84.0 0.7 copy-done
  84.7 0.1 copy-done.2
  84.8 0.2 pad_maximum_fusion
  85.0 0.0 all-gather.6.cloned.1.call-done
  85.0 2.8 %fusion.9 = (bf16[512,256]{1,0:T(8,128)(2,1)S(1)}, f32[512,256]{1,0:T(8,128)S(1)}) fusion(bf16[512,2304]{1,0:T(8,128)(2,1)} %bitcast.65, bf16[2304,768]{1,0:T(8,128)(2,1)} %all-gather.6.cloned.1.call-done), kind=kOutput, calls=%fused_computation.46 | convolution fusion | flops 604110848 | bytes 4325376 | tf_op jit(solution)/shard_map/dot_general | solution.py:227
  87.8 7.4 %all-gather.1 = bf16[1024,256]{1,0:T(8,128)(2,1)S(1)} all-gather(bf16[512,256]{1,0:T(8,128)(2,1)S(1)} %get-tuple-element.46), channel_id=3, replica_groups=mesh['xh'=2,'z'=16,'xl'=2,'y'=4,'c'=2] {'xh'}, dimensions={0}, use_global_device_ids=true | all-gather | bytes 786432 | tf_op jit(solution)/shard_map/all_gather | solution.py:230
  95.2 0.8 shard_map.82
  96.1 0.5 slice-done
  96.5 0.2 broadcast_in_dim.83
  96.7 20.7 %all_to_all.42 = bf16[2,1,2304,256]{3,2,1,0:T(8,128)(2,1)S(1)} all-to-all(bf16[2,1,2304,256]{3,2,1,0:T(8,128)(2,1)S(1)} %broadcast_in_dim.83), channel_id=1, replica_groups=mesh['xh'=2,'z'=16,'xl'=2,'y'=4,'c'=2] {'xh'}, dimensions={0} | all-to-all | bytes 4718592 | tf_op jit(solution)/shard_map/all_to_all | solution.py:24
  117.4 13.8 %collective-permute-start.1 = (bf16[4608,256]{1,0:T(8,128)(2,1)S(1)}, bf16[4608,256]{1,0:T(8,128)(2,1)}, u32[]{:S(2)}, u32[]{:S(2)}) collective-permute-start(bf16[4608,256]{1,0:T(8,128)(2,1)S(1)} %bitcast.58), channel_id=1, source_target_pairs={{0,1},{1,0},{2,3},{3,2},{4,5},{5,4},{6,7},{7,6},{8,9},{9,8},{10,11... | collective-permute-start | bytes 7077896 | tf_op jit(solution)/shard_map/ppermute | solution.py:250
  131.3 0.6 slice.49
  134.4 3.6 %fusion.2 = f32[512,256]{1,0:T(8,128)} fusion(bf16[512,2304]{1,0:T(8,128)(2,1)} %bitcast.66, bf16[2304,768]{1,0:T(8,128)(2,1)} %all-gather.6.cloned.1.call-done), kind=kOutput, calls=%fused_computation.8 | convolution fusion | flops 603979776 | bytes 4063232 | tf_op jit(solution)/shard_map/dot_general | solution.py:227
  138.1 3.5 %all-to-all-start.4 = ((f32[2,256,256]{2,1,0:T(8,128)}), f32[2,256,256]{2,1,0:T(8,128)S(1)}, u32[]{:S(2)}, u32[]{:S(2)}) async-start(f32[2,256,256]{2,1,0:T(8,128)} %bitcast.71), calls=%async_computation.4 | async-start | bytes 1048576 | tf_op jit(solution)/shard_map/all_to_all | solution.py:236
  141.6 0.9 copy.41
  142.5 0.6 pad_add_fusion.where_ref
  143.1 8.0 %all-to-all-done.4 = f32[2,256,256]{2,1,0:T(8,128)S(1)} async-done(((f32[2,256,256]{2,1,0:T(8,128)}), f32[2,256,256]{2,1,0:T(8,128)S(1)}, u32[]{:S(2)}, u32[]{:S(2)}) %all-to-all-start.4) | async-done | bytes 524320 | tf_op jit(solution)/shard_map/all_to_all | solution.py:236
  151.1 1.0 multiply_subtract_fusion.1
  152.2 0.1 fusion.7
  152.3 0.1 fusion.6
  152.4 0.7 pad_maximum_fusion.4.query_ref
  153.1 19.0 %all-gather.8.cloned.1.call-done.kv_hbm = bf16[8192,256]{1,0:T(8,128)(2,1)} async-done(((bf16[512,256]{1,0:T(8,128)(2,1)}), bf16[8192,256]{1,0:T(8,128)(2,1)}) %all-gather.8.cloned.1.call-update) | async-done | bytes 4194320 | tf_op jit(solution)/shard_map/all_gather | solution.py:233
  172.0 3.5 %shard_map.83 = (bf16[128,256]{1,0:T(8,128)(2,1)}, bf16[128,256]{1,0:T(8,128)(2,1)}) custom-call(s32[4]{0:T(128)} %pad_add_fusion.where_ref, bf16[512,128]{1,0:T(8,128)(2,1)} %pad_maximum_fusion.4.query_ref, s32[512,1]{1,0:T(8,128)} %bitcast.72, bf16[8192,256]{1,0:T(8,128)(2,1)} %all-gather.8.cloned.1.call-done.kv_hbm), custom_call_target="tpu_custom_call" | custom-call | flops 1073741824 | bytes 2097152 | tf_op jit(solution)/shard_map/pallas_call | solution.py:126
  175.5 11.0 %collective-permute-start.2 = (bf16[128,256]{1,0:T(8,128)(2,1)}, bf16[128,256]{1,0:T(8,128)(2,1)S(1)}, u32[]{:S(2)}, u32[]{:S(2)}) collective-permute-start(bf16[128,256]{1,0:T(8,128)(2,1)} %get-tuple-element.35), channel_id=1, source_target_pairs={{0,1},{1,0},{2,3},{3,2},{4,5},{5,4},{6,7},{7,6},{8,9},{9,8},{10,11... | collective-permute-start | bytes 196616 | tf_op jit(solution)/shard_map/ppermute | solution.py:254
  186.5 1.7 fusion.10
  188.3 2.6 %fusion.11 = f32[128,4608]{1,0:T(8,128)S(1)} fusion(bf16[128,256]{1,0:T(8,128)(2,1)S(1)} %collective-permute-done.2, bf16[4608,256]{1,0:T(8,128)(2,1)} %collective-permute-done.1), kind=kOutput, calls=%fused_computation.48 | convolution fusion | flops 301989888 | bytes 4784128 | tf_op jit(solution)/shard_map/dot_general | solution.py:257
  190.8 0.2 add_convert_fusion
  191.1 21.4 %all_to_all.43 = bf16[8,16,4608]{2,1,0:T(8,128)(2,1)S(1)} all-to-all(bf16[8,16,4608]{2,1,0:T(8,128)(2,1)S(1)} %bitcast.64), channel_id=1, replica_groups=mesh['xh'=2,'z'=16,'xl'=2,'y'=4,'c'=2] {'xl','y'}, dimensions={0} | all-to-all | bytes 2359296 | tf_op jit(solution)/shard_map/all_to_all | solution.py:264
  212.4 0.2 convert_reduce_fusion
  212.6 0.2 multiply_reduce_fusion.1
  212.8 0.1 add_convert_fusion.1
  212.9 0.1 broadcast_in_dim.84
  213.0 19.7 %all_to_all.44 = bf16[8,16,4608]{2,1,0:T(8,128)(2,1)S(1)} all-to-all(bf16[8,16,4608]{2,1,0:T(8,128)(2,1)S(1)} %broadcast_in_dim.84), channel_id=1, replica_groups=mesh['xh'=2,'z'=16,'xl'=2,'y'=4,'c'=2] {'xl','y'}, dimensions={0} | all-to-all | bytes 2359296 | tf_op jit(solution)/shard_map/all_to_all | solution.py:24
  232.7 3.8 %collective-permute-start.3 = (bf16[128,4608]{1,0:T(8,128)(2,1)S(1)}, bf16[128,4608]{1,0:T(8,128)(2,1)S(1)}, u32[]{:S(2)}, u32[]{:S(2)}) collective-permute-start(bf16[128,4608]{1,0:T(8,128)(2,1)S(1)} %bitcast.62), channel_id=1, source_target_pairs={{0,1},{1,0},{2,3},{3,2},{4,5},{5,4},{6,7},{7,6},{8,9},{9,8},{10,11... | collective-permute-start | bytes 3538952 | tf_op jit(solution)/shard_map/ppermute | solution.py:269
  236.6 0.1 broadcast_bitcast_fusion.1
  236.7 2.4 collective-permute-done.3
  239.0 1.7 bitcast_select_fusion
  (34 shorter events, 0.3 us)
Async XLA Ops:
  6.5 78.5 %all-gather.6.cloned.1.call-start = ((), (), s32[]{:S(2)}) async-start(), calls=%async_computation.8 | async-start | bytes 3760128 | tf_op jit(solution)/shard_map/all_gather | solution.py:175
  9.8 17.9 %collective-permute-start = (bf16[304,256]{1,0:T(8,128)(2,1)S(1)}, bf16[304,256]{1,0:T(8,128)(2,1)S(1)}, u32[]{:S(2)}, u32[]{:S(2)}) collective-permute-start(bf16[304,256]{1,0:T(8,128)(2,1)S(1)} %pad_maximum_fusion.3), channel_id=1, source_target_pairs={{0,0},{8,256},{256,8},{264,264},{1,1},{9,257},{257,9},{265,265},{2... | collective-permute-start | bytes 466952 | tf_op jit(solution)/shard_map/ppermute | solution.py:180
  11.6 20.8 %copy-start.5 = (f32[4608]{0:T(1024)S(1)}, f32[4608]{0:T(1024)}, u32[]{:S(2)}) copy-start(f32[4608]{0:T(1024)} %param.10) | copy-start | bytes 55300
  28.8 20.7 %all-to-all-start = ((bf16[8,1,304,256]{3,2,1,0:T(8,128)(2,1)}), bf16[8,1,304,256]{3,2,1,0:T(8,128)(2,1)S(1)}, u32[]{:S(2)}, u32[]{:S(2)}) async-start(bf16[8,1,304,256]{3,2,1,0:T(8,128)(2,1)} %broadcast_in_dim.79), calls=%async_computation | async-start | bytes 2490368 | tf_op jit(solution)/shard_map/all_to_all | solution.py:24
  56.6 26.2 %all-to-all-start.2 = ((f32[16,1,8]{2,1,0:T(1,128)}), f32[16,1,8]{2,1,0:T(1,128)S(1)}, u32[]{:S(2)}, u32[]{:S(2)}) async-start(f32[16,1,8]{2,1,0:T(1,128)} %broadcast_in_dim.81), calls=%async_computation.2 | async-start | bytes 16384 | tf_op jit(solution)/shard_map/all_to_all | solution.py:24
  71.5 100.5 %all-gather.8.cloned.1.call-start = ((), (), s32[]{:S(2)}) async-start(), calls=%async_computation.9 | async-start | bytes 4456448 | tf_op jit(solution)/shard_map/all_gather | solution.py:233
  84.0 0.7 copy-start
  84.0 0.8 copy-start.2
  95.2 1.4 slice-start
  117.4 35.6 %collective-permute-start.1 = (bf16[4608,256]{1,0:T(8,128)(2,1)S(1)}, bf16[4608,256]{1,0:T(8,128)(2,1)}, u32[]{:S(2)}, u32[]{:S(2)}) collective-permute-start(bf16[4608,256]{1,0:T(8,128)(2,1)S(1)} %bitcast.58), channel_id=1, source_target_pairs={{0,1},{1,0},{2,3},{3,2},{4,5},{5,4},{6,7},{7,6},{8,9},{9,8},{10,11... | collective-permute-start | bytes 7077896 | tf_op jit(solution)/shard_map/ppermute | solution.py:250
  134.4 16.7 %copy-start.1 = (f32[512,64]{1,0:T(8,128)S(1)}, f32[512,64]{1,0:T(8,128)}, u32[]{:S(2)}) copy-start(f32[512,64]{1,0:T(8,128)} %copy-done) | copy-start | bytes 393220
  138.1 13.0 %all-to-all-start.4 = ((f32[2,256,256]{2,1,0:T(8,128)}), f32[2,256,256]{2,1,0:T(8,128)S(1)}, u32[]{:S(2)}, u32[]{:S(2)}) async-start(f32[2,256,256]{2,1,0:T(8,128)} %bitcast.71), calls=%async_computation.4 | async-start | bytes 1048576 | tf_op jit(solution)/shard_map/all_to_all | solution.py:236
  175.5 12.7 %collective-permute-start.2 = (bf16[128,256]{1,0:T(8,128)(2,1)}, bf16[128,256]{1,0:T(8,128)(2,1)S(1)}, u32[]{:S(2)}, u32[]{:S(2)}) collective-permute-start(bf16[128,256]{1,0:T(8,128)(2,1)} %get-tuple-element.35), channel_id=1, source_target_pairs={{0,1},{1,0},{2,3},{3,2},{4,5},{5,4},{6,7},{7,6},{8,9},{9,8},{10,11... | collective-permute-start | bytes 196616 | tf_op jit(solution)/shard_map/ppermute | solution.py:254
  191.0 21.7 %copy-start.3 = (bf16[16,4608]{1,0:T(8,128)(2,1)S(1)}, bf16[16,4608]{1,0:T(8,128)(2,1)}, u32[]{:S(2)}) copy-start(bf16[16,4608]{1,0:T(8,128)(2,1)} %reshape.112) | copy-start | bytes 442372
  191.1 21.7 %copy-start.4 = (f32[4608]{0:T(1024)S(1)}, f32[4608]{0:T(1024)}, u32[]{:S(2)}) copy-start(f32[4608]{0:T(1024)} %param.11) | copy-start | bytes 55300
  232.7 6.3 %collective-permute-start.3 = (bf16[128,4608]{1,0:T(8,128)(2,1)S(1)}, bf16[128,4608]{1,0:T(8,128)(2,1)S(1)}, u32[]{:S(2)}, u32[]{:S(2)}) collective-permute-start(bf16[128,4608]{1,0:T(8,128)(2,1)S(1)} %bitcast.62), channel_id=1, source_target_pairs={{0,1},{1,0},{2,3},{3,2},{4,5},{5,4},{6,7},{7,6},{8,9},{9,8},{10,11... | collective-permute-start | bytes 3538952 | tf_op jit(solution)/shard_map/ppermute | solution.py:269
Sparse Core Ops, SparseCore 0:
  9.4 73.2 all-gather.5
  96.2 75.8 all-gather.7

commit v4 on v3

--- a/solution.py
+++ b/solution.py
@@ -77,7 +77,7 @@
         add(weigh(keys), values)
 
     done = low + 1
-    for count in (4, 2, 1):
+    for count in (5, 2, 1):
         steps = lax.div(jnp.maximum(own - done, 0), count)
 
         @pl.loop(0, steps)

time: 249 us -> 251 us (level)
  no operation moved by 1% of the time
where the time goes in v4:
time: 251 us; the launch traced here: 248 us
  blocking collectives  96.1 us (38%)
  starting transfers between devices  51.3 us (20%)
  waiting for transfers between devices  47.7 us (19%)
  between operations  16.3 us (6%)
  other arithmetic  11.5 us (5%)
  matrix products  10.7 us (4%)
  local copies, waits for them, and re-layouts  9.62 us (4%)
  Pallas kernels  4.33 us (2%)
    all_to_all x3, blocking collectives, from_everyone(): return lax.all_to_all(copies, axis, split_axis=0, concat_axis=0, tiled=True)  46.5 us
    all_to_all x1, blocking collectives, local(): lax.all_to_all(halves.reshape(near, few, D), PLANE, 0, 0, tiled=True)  21.4 us
    all_gather x1, waiting for transfers between devices, local(): kv_all = lax.all_gather(kv_pair, 'z', axis=0, tiled=True)  19 us
    all_to_all x2, starting transfers between devices, from_everyone(): return lax.all_to_all(copies, axis, split_axis=0, concat_axis=0, tiled=True)  18.5 us
    all_to_all x2, waiting for transfers between devices, from_everyone(): return lax.all_to_all(copies, axis, split_axis=0, concat_axis=0, tiled=True)  18.3 us
    all_to_all x1, blocking collectives, local(): lax.all_to_all(pieces, HEAD, 0, 0, tiled=True).transpose(1, 0, 2)  16.1 us
    ppermute x1, starting transfers between devices, local(): out_far = lax.ppermute(out_t, 'c', swap)  13.8 us
    ppermute x1, starting transfers between devices, local(): far = lax.ppermute(away, 'c', swap)  11 us
  transfers between devices with their start and end apart: 9, of which 5 were waited for; matrix products, arithmetic and copies ran while one was open for 9% of the time, Pallas kernels for 0%

profile of v4, /device:TPU:1, one launch (start us, length us, event | category | flops | bytes accessed | tf_op | source)
XLA Modules:
  0.0 247.5 jit_solution(16859229077214915148)
XLA Ops:
  6.5 1.6 pad_maximum_fusion.2
  8.2 0.7 convert_element_type.71
  8.9 0.9 pad_maximum_fusion.3
  9.8 0.7 collective-permute-start
  10.5 1.1 copy.33
  11.6 16.1 %all_to_all.40 = bf16[16,16,288]{2,1,0:T(8,128)(2,1)S(1)} all-to-all(bf16[16,16,288]{2,1,0:T(8,128)(2,1)S(1)} %bitcast.68), channel_id=1, replica_groups=mesh['xh'=2,'z'=16,'xl'=2,'y'=4,'c'=2] {'xl','y','c'}, dimensions={0} | all-to-all | bytes 294912 | tf_op jit(solution)/shard_map/all_to_all | solution.py:219
  27.7 1.1 broadcast_in_dim.79
  28.8 3.6 %all-to-all-start = ((bf16[8,1,304,256]{3,2,1,0:T(8,128)(2,1)}), bf16[8,1,304,256]{3,2,1,0:T(8,128)(2,1)S(1)}, u32[]{:S(2)}, u32[]{:S(2)}) async-start(bf16[8,1,304,256]{3,2,1,0:T(8,128)(2,1)} %broadcast_in_dim.79), calls=%async_computation | async-start | bytes 2490368 | tf_op jit(solution)/shard_map/all_to_all | solution.py:24
  32.4 0.1 dynamic_slice.13
  32.6 0.9 reshape.112
  33.4 16.1 %all-to-all-done = bf16[8,1,304,256]{3,2,1,0:T(8,128)(2,1)S(1)} async-done(((bf16[8,1,304,256]{3,2,1,0:T(8,128)(2,1)}), bf16[8,1,304,256]{3,2,1,0:T(8,128)(2,1)S(1)}, u32[]{:S(2)}, u32[]{:S(2)}) %all-to-all-start) | async-done | bytes 1245216 | tf_op jit(solution)/shard_map/all_to_all | solution.py:24
  49.5 0.2 broadcast_in_dim.80
  49.7 6.0 %all_to_all.41 = bf16[2,1,8,304,256]{4,3,2,1,0:T(8,128)(2,1)S(1)} all-to-all(bf16[2,1,8,304,256]{4,3,2,1,0:T(8,128)(2,1)S(1)} %broadcast_in_dim.80), channel_id=1, replica_groups=mesh['xh'=2,'z'=16,'xl'=2,'y'=4,'c'=2] {'c'}, dimensions={0} | all-to-all | bytes 4980736 | tf_op jit(solution)/shard_map/all_to_all | solution.py:24
  55.7 0.2 copy.30
  55.9 0.1 convert_reduce_fusion.1
  56.0 0.6 broadcast_in_dim.81
  56.6 14.9 %all-to-all-start.2 = ((f32[16,1,8]{2,1,0:T(1,128)}), f32[16,1,8]{2,1,0:T(1,128)S(1)}, u32[]{:S(2)}, u32[]{:S(2)}) async-start(f32[16,1,8]{2,1,0:T(1,128)} %broadcast_in_dim.81), calls=%async_computation.2 | async-start | bytes 16384 | tf_op jit(solution)/shard_map/all_to_all | solution.py:24
  71.5 0.0 all-gather.8.cloned.1.call-start
  71.6 0.5 multiply_reduce_fusion
  72.1 4.7 %all-gather.2 = f32[2,2,256]{2,1,0:T(2,128)S(1)} all-gather(f32[1,2,256]{2,1,0:T(2,128)S(1)} %bitcast.78), channel_id=2, replica_groups=mesh['xh'=2,'z'=16,'xl'=2,'y'=4,'c'=2] {'xh'}, dimensions={0}, use_global_device_ids=true | all-gather | bytes 6144 | tf_op jit(solution)/shard_map/all_gather | solution.py:211
  76.8 0.5 slice_convert_fusion
  77.3 0.8 fusion.1
  78.1 2.4 copy.31
  80.6 2.2 all-to-all-done.2
  82.8 0.1 select_reduce_fusion
  82.9 0.1 subtract_bitcast_fusion
  83.0 1.0 fusion.8
  84.0 0.7 copy-done
  84.7 0.1 copy-done.2
  84.8 0.2 pad_maximum_fusion
  85.0 0.0 all-gather.6.cloned.1.call-done
  85.0 2.8 %fusion.9 = (bf16[512,256]{1,0:T(8,128)(2,1)S(1)}, f32[512,256]{1,0:T(8,128)S(1)}) fusion(bf16[512,2304]{1,0:T(8,128)(2,1)} %bitcast.65, bf16[2304,768]{1,0:T(8,128)(2,1)} %all-gather.6.cloned.1.call-done), kind=kOutput, calls=%fused_computation.46 | convolution fusion | flops 604110848 | bytes 4325376 | tf_op jit(solution)/shard_map/dot_general | solution.py:227
  87.8 7.4 %all-gather.1 = bf16[1024,256]{1,0:T(8,128)(2,1)S(1)} all-gather(bf16[512,256]{1,0:T(8,128)(2,1)S(1)} %get-tuple-element.46), channel_id=3, replica_groups=mesh['xh'=2,'z'=16,'xl'=2,'y'=4,'c'=2] {'xh'}, dimensions={0}, use_global_device_ids=true | all-gather | bytes 786432 | tf_op jit(solution)/shard_map/all_gather | solution.py:230
  95.2 0.8 shard_map.82
  96.1 0.5 slice-done
  96.5 0.2 broadcast_in_dim.83
  96.7 20.7 %all_to_all.42 = bf16[2,1,2304,256]{3,2,1,0:T(8,128)(2,1)S(1)} all-to-all(bf16[2,1,2304,256]{3,2,1,0:T(8,128)(2,1)S(1)} %broadcast_in_dim.83), channel_id=1, replica_groups=mesh['xh'=2,'z'=16,'xl'=2,'y'=4,'c'=2] {'xh'}, dimensions={0} | all-to-all | bytes 4718592 | tf_op jit(solution)/shard_map/all_to_all | solution.py:24
  117.4 13.8 %collective-permute-start.1 = (bf16[4608,256]{1,0:T(8,128)(2,1)S(1)}, bf16[4608,256]{1,0:T(8,128)(2,1)}, u32[]{:S(2)}, u32[]{:S(2)}) collective-permute-start(bf16[4608,256]{1,0:T(8,128)(2,1)S(1)} %bitcast.58), channel_id=1, source_target_pairs={{0,1},{1,0},{2,3},{3,2},{4,5},{5,4},{6,7},{7,6},{8,9},{9,8},{10,11... | collective-permute-start | bytes 7077896 | tf_op jit(solution)/shard_map/ppermute | solution.py:250
  131.3 0.6 slice.49
  134.4 3.6 %fusion.2 = f32[512,256]{1,0:T(8,128)} fusion(bf16[512,2304]{1,0:T(8,128)(2,1)} %bitcast.66, bf16[2304,768]{1,0:T(8,128)(2,1)} %all-gather.6.cloned.1.call-done), kind=kOutput, calls=%fused_computation.8 | convolution fusion | flops 603979776 | bytes 4063232 | tf_op jit(solution)/shard_map/dot_general | solution.py:227
  138.1 3.5 %all-to-all-start.4 = ((f32[2,256,256]{2,1,0:T(8,128)}), f32[2,256,256]{2,1,0:T(8,128)S(1)}, u32[]{:S(2)}, u32[]{:S(2)}) async-start(f32[2,256,256]{2,1,0:T(8,128)} %bitcast.71), calls=%async_computation.4 | async-start | bytes 1048576 | tf_op jit(solution)/shard_map/all_to_all | solution.py:236
  141.6 0.9 copy.41
  142.5 0.6 pad_add_fusion.where_ref
  143.1 8.0 %all-to-all-done.4 = f32[2,256,256]{2,1,0:T(8,128)S(1)} async-done(((f32[2,256,256]{2,1,0:T(8,128)}), f32[2,256,256]{2,1,0:T(8,128)S(1)}, u32[]{:S(2)}, u32[]{:S(2)}) %all-to-all-start.4) | async-done | bytes 524320 | tf_op jit(solution)/shard_map/all_to_all | solution.py:236
  151.1 1.0 multiply_subtract_fusion.1
  152.2 0.1 fusion.7
  152.3 0.1 fusion.6
  152.4 0.7 pad_maximum_fusion.4.query_ref
  153.1 19.0 %all-gather.8.cloned.1.call-done.kv_hbm = bf16[8192,256]{1,0:T(8,128)(2,1)} async-done(((bf16[512,256]{1,0:T(8,128)(2,1)}), bf16[8192,256]{1,0:T(8,128)(2,1)}) %all-gather.8.cloned.1.call-update) | async-done | bytes 4194320 | tf_op jit(solution)/shard_map/all_gather | solution.py:233
  172.0 3.5 %shard_map.83 = (bf16[128,256]{1,0:T(8,128)(2,1)}, bf16[128,256]{1,0:T(8,128)(2,1)}) custom-call(s32[4]{0:T(128)} %pad_add_fusion.where_ref, bf16[512,128]{1,0:T(8,128)(2,1)} %pad_maximum_fusion.4.query_ref, s32[512,1]{1,0:T(8,128)} %bitcast.72, bf16[8192,256]{1,0:T(8,128)(2,1)} %all-gather.8.cloned.1.call-done.kv_hbm), custom_call_target="tpu_custom_call" | custom-call | flops 1073741824 | bytes 2097152 | tf_op jit(solution)/shard_map/pallas_call | solution.py:126
  175.5 11.0 %collective-permute-start.2 = (bf16[128,256]{1,0:T(8,128)(2,1)}, bf16[128,256]{1,0:T(8,128)(2,1)S(1)}, u32[]{:S(2)}, u32[]{:S(2)}) collective-permute-start(bf16[128,256]{1,0:T(8,128)(2,1)} %get-tuple-element.35), channel_id=1, source_target_pairs={{0,1},{1,0},{2,3},{3,2},{4,5},{5,4},{6,7},{7,6},{8,9},{9,8},{10,11... | collective-permute-start | bytes 196616 | tf_op jit(solution)/shard_map/ppermute | solution.py:254
  186.5 1.7 fusion.10
  188.3 2.6 %fusion.11 = f32[128,4608]{1,0:T(8,128)S(1)} fusion(bf16[128,256]{1,0:T(8,128)(2,1)S(1)} %collective-permute-done.2, bf16[4608,256]{1,0:T(8,128)(2,1)} %collective-permute-done.1), kind=kOutput, calls=%fused_computation.48 | convolution fusion | flops 301989888 | bytes 4784128 | tf_op jit(solution)/shard_map/dot_general | solution.py:257
  190.8 0.2 add_convert_fusion
  191.1 21.4 %all_to_all.43 = bf16[8,16,4608]{2,1,0:T(8,128)(2,1)S(1)} all-to-all(bf16[8,16,4608]{2,1,0:T(8,128)(2,1)S(1)} %bitcast.64), channel_id=1, replica_groups=mesh['xh'=2,'z'=16,'xl'=2,'y'=4,'c'=2] {'xl','y'}, dimensions={0} | all-to-all | bytes 2359296 | tf_op jit(solution)/shard_map/all_to_all | solution.py:264
  212.4 0.2 convert_reduce_fusion
  212.6 0.2 multiply_reduce_fusion.1
  212.8 0.1 add_convert_fusion.1
  212.9 0.1 broadcast_in_dim.84
  213.0 19.7 %all_to_all.44 = bf16[8,16,4608]{2,1,0:T(8,128)(2,1)S(1)} all-to-all(bf16[8,16,4608]{2,1,0:T(8,128)(2,1)S(1)} %broadcast_in_dim.84), channel_id=1, replica_groups=mesh['xh'=2,'z'=16,'xl'=2,'y'=4,'c'=2] {'xl','y'}, dimensions={0} | all-to-all | bytes 2359296 | tf_op jit(solution)/shard_map/all_to_all | solution.py:24
  232.7 3.8 %collective-permute-start.3 = (bf16[128,4608]{1,0:T(8,128)(2,1)S(1)}, bf16[128,4608]{1,0:T(8,128)(2,1)S(1)}, u32[]{:S(2)}, u32[]{:S(2)}) collective-permute-start(bf16[128,4608]{1,0:T(8,128)(2,1)S(1)} %bitcast.62), channel_id=1, source_target_pairs={{0,1},{1,0},{2,3},{3,2},{4,5},{5,4},{6,7},{7,6},{8,9},{9,8},{10,11... | collective-permute-start | bytes 3538952 | tf_op jit(solution)/shard_map/ppermute | solution.py:269
  236.6 0.1 broadcast_bitcast_fusion.1
  236.7 2.4 collective-permute-done.3
  239.0 1.7 bitcast_select_fusion
  (34 shorter events, 0.3 us)
Async XLA Ops:
  6.5 78.5 %all-gather.6.cloned.1.call-start = ((), (), s32[]{:S(2)}) async-start(), calls=%async_computation.8 | async-start | bytes 3760128 | tf_op jit(solution)/shard_map/all_gather | solution.py:175
  9.8 17.9 %collective-permute-start = (bf16[304,256]{1,0:T(8,128)(2,1)S(1)}, bf16[304,256]{1,0:T(8,128)(2,1)S(1)}, u32[]{:S(2)}, u32[]{:S(2)}) collective-permute-start(bf16[304,256]{1,0:T(8,128)(2,1)S(1)} %pad_maximum_fusion.3), channel_id=1, source_target_pairs={{0,0},{8,256},{256,8},{264,264},{1,1},{9,257},{257,9},{265,265},{2... | collective-permute-start | bytes 466952 | tf_op jit(solution)/shard_map/ppermute | solution.py:180
  11.6 20.8 %copy-start.5 = (f32[4608]{0:T(1024)S(1)}, f32[4608]{0:T(1024)}, u32[]{:S(2)}) copy-start(f32[4608]{0:T(1024)} %param.10) | copy-start | bytes 55300
  28.8 20.7 %all-to-all-start = ((bf16[8,1,304,256]{3,2,1,0:T(8,128)(2,1)}), bf16[8,1,304,256]{3,2,1,0:T(8,128)(2,1)S(1)}, u32[]{:S(2)}, u32[]{:S(2)}) async-start(bf16[8,1,304,256]{3,2,1,0:T(8,128)(2,1)} %broadcast_in_dim.79), calls=%async_computation | async-start | bytes 2490368 | tf_op jit(solution)/shard_map/all_to_all | solution.py:24
  56.6 26.2 %all-to-all-start.2 = ((f32[16,1,8]{2,1,0:T(1,128)}), f32[16,1,8]{2,1,0:T(1,128)S(1)}, u32[]{:S(2)}, u32[]{:S(2)}) async-start(f32[16,1,8]{2,1,0:T(1,128)} %broadcast_in_dim.81), calls=%async_computation.2 | async-start | bytes 16384 | tf_op jit(solution)/shard_map/all_to_all | solution.py:24
  71.5 100.5 %all-gather.8.cloned.1.call-start = ((), (), s32[]{:S(2)}) async-start(), calls=%async_computation.9 | async-start | bytes 4456448 | tf_op jit(solution)/shard_map/all_gather | solution.py:233
  84.0 0.7 copy-start
  84.0 0.8 copy-start.2
  95.2 1.4 slice-start
  117.4 35.6 %collective-permute-start.1 = (bf16[4608,256]{1,0:T(8,128)(2,1)S(1)}, bf16[4608,256]{1,0:T(8,128)(2,1)}, u32[]{:S(2)}, u32[]{:S(2)}) collective-permute-start(bf16[4608,256]{1,0:T(8,128)(2,1)S(1)} %bitcast.58), channel_id=1, source_target_pairs={{0,1},{1,0},{2,3},{3,2},{4,5},{5,4},{6,7},{7,6},{8,9},{9,8},{10,11... | collective-permute-start | bytes 7077896 | tf_op jit(solution)/shard_map/ppermute | solution.py:250
  134.4 16.7 %copy-start.1 = (f32[512,64]{1,0:T(8,128)S(1)}, f32[512,64]{1,0:T(8,128)}, u32[]{:S(2)}) copy-start(f32[512,64]{1,0:T(8,128)} %copy-done) | copy-start | bytes 393220
  138.1 13.0 %all-to-all-start.4 = ((f32[2,256,256]{2,1,0:T(8,128)}), f32[2,256,256]{2,1,0:T(8,128)S(1)}, u32[]{:S(2)}, u32[]{:S(2)}) async-start(f32[2,256,256]{2,1,0:T(8,128)} %bitcast.71), calls=%async_computation.4 | async-start | bytes 1048576 | tf_op jit(solution)/shard_map/all_to_all | solution.py:236
  175.5 12.7 %collective-permute-start.2 = (bf16[128,256]{1,0:T(8,128)(2,1)}, bf16[128,256]{1,0:T(8,128)(2,1)S(1)}, u32[]{:S(2)}, u32[]{:S(2)}) collective-permute-start(bf16[128,256]{1,0:T(8,128)(2,1)} %get-tuple-element.35), channel_id=1, source_target_pairs={{0,1},{1,0},{2,3},{3,2},{4,5},{5,4},{6,7},{7,6},{8,9},{9,8},{10,11... | collective-permute-start | bytes 196616 | tf_op jit(solution)/shard_map/ppermute | solution.py:254
  191.0 21.7 %copy-start.3 = (bf16[16,4608]{1,0:T(8,128)(2,1)S(1)}, bf16[16,4608]{1,0:T(8,128)(2,1)}, u32[]{:S(2)}) copy-start(bf16[16,4608]{1,0:T(8,128)(2,1)} %reshape.112) | copy-start | bytes 442372
  191.1 21.7 %copy-start.4 = (f32[4608]{0:T(1024)S(1)}, f32[4608]{0:T(1024)}, u32[]{:S(2)}) copy-start(f32[4608]{0:T(1024)} %param.11) | copy-start | bytes 55300
  232.7 6.3 %collective-permute-start.3 = (bf16[128,4608]{1,0:T(8,128)(2,1)S(1)}, bf16[128,4608]{1,0:T(8,128)(2,1)S(1)}, u32[]{:S(2)}, u32[]{:S(2)}) collective-permute-start(bf16[128,4608]{1,0:T(8,128)(2,1)S(1)} %bitcast.62), channel_id=1, source_target_pairs={{0,1},{1,0},{2,3},{3,2},{4,5},{5,4},{6,7},{7,6},{8,9},{9,8},{10,11... | collective-permute-start | bytes 3538952 | tf_op jit(solution)/shard_map/ppermute | solution.py:269
Sparse Core Ops, SparseCore 0:
  9.4 73.2 all-gather.5
  96.2 75.8 all-gather.7
